TPU v7x, 32 devices: a whole 2x2x4 slice. The times are simulated.
32 devices in a mesh: dp: 4 (over y, x), context: 4 (over z), head: 2 (over core).
Axes of the slice: x: 2, y: 2, z: 4, core: 2. Of those that a mesh axis runs over, the one named last changes fastest.
Arguments:
- tokens: bfloat16 [4, 2, 512, 4096], P('dp', None, 'context', 'head'), may hold values from -7 to 7
- queries: bfloat16 [4, 2, 512, 2048], P('dp', None, 'context', 'head'), may hold values from -160 to 160
- grad_out: bfloat16 [4, 2, 512, 2048], P('dp', None, 'context', 'head'), may hold values from -6 to 6
- w_key: bfloat16 [4096, 256], P('context', 'head'), may hold values from -0.09375 to 0.09375
- w_value: bfloat16 [4096, 256], P('context', 'head'), may hold values from -0.09375 to 0.09375
- block_len: int32 [4], P('dp'), may hold values from 8 to 32, as said below
Outputs:
- grad_query: bfloat16 [4, 2, 512, 2048], P('dp', None, 'context', 'head')
- grad_x: bfloat16 [4, 2, 512, 4096], P('dp', None, 'context', 'head')
- grad_wkey: float32 [4096, 256], P('context', 'head')
- grad_wvalue: float32 [4096, 256], P('context', 'head')
Inputs may be any that keep to these rules, and one draw needn't show every extreme that they name: `block_len`: each entry is 8, 16 or 32.
All inputs are finite; a program needn't handle non-finite values.
Results may differ from a plain program's by a relative error of at most 0.025.
Values may be sent and summed in bfloat16 or wider, within the bound.
A program may use at most 64 MiB of HBM per device.

v0:
```python
import functools
import math

import jax
import jax.numpy as jnp
from jax import lax
from jax.experimental import pallas as pl
from jax.experimental.pallas import tpu as pltpu
from jax.sharding import PartitionSpec as P

HEAD_DIM = 128
MASKED = -1e30
MESH = pl.DeviceIdType.MESH
NT = (((1,), (1,)), ((), ()))


def near_first(count):
    order = []
    for step in range(1, count):
        for offset in (step, count - step):
            if offset not in order:
                order.append(offset)
    return order


def dot(left, right):
    return jnp.dot(left, right, preferred_element_type=jnp.float32)


def dot_nt(left, right):
    return lax.dot_general(left, right, NT, preferred_element_type=jnp.float32)


def fused_kernel(
    n, m, share, early,
    blk_ref, tok_ref, q_ref, g_ref, wk_ref, wv_ref,
    dq_ref, gx_ref, gwk_ref, gwv_ref,
    tokf, wf, wo, kv, kvn, kt, knt, dkv, dn, pgp, pin, pga, pgo, tokd, gsum, rp, rin, rall,
    loc_sem, tok_sem, wz_s, wz_r, wd_s, wd_r, wx_s, wx_r, wo_sem, kv_s, kv_r,
    td_s, td_r, tf_s, tf_r, pp_s, pp_r, pn_s, pn_r, pc_s, pc_r, po_sem, rs_s, rs_r, ra_s, ra_r,
):
    me_dp = lax.axis_index("dp")
    me = lax.axis_index("context")
    head = lax.axis_index("head")
    other = 1 - head
    rows2, features = tok_ref.shape
    rows = rows2 // 2
    wrows = wk_ref.shape[0]
    half = n // 2
    score_scale = 1.0 / math.sqrt(HEAD_DIM)
    sends = []

    def copy_of(src, dst, send_sem, recv_sem, **device):
        return pltpu.make_async_remote_copy(
            src_ref=src, dst_ref=dst, send_sem=send_sem, recv_sem=recv_sem,
            device_id=device, device_id_type=MESH,
        )

    def put(src, dst, send_sem, recv_sem, **device):
        copy = copy_of(src, dst, send_sem, recv_sem, **device)
        copy.start()
        sends.append((None, copy))

    def put_if(condition, src, dst, send_sem, recv_sem, **device):
        copy = copy_of(src, dst, send_sem, recv_sem, **device)
        pl.when(condition)(copy.start)
        sends.append((condition, copy))

    def arrived(dst, send_sem, recv_sem):
        copy_of(dst, dst, send_sem, recv_sem, head=other).wait_recv()

    ctx_peers = [(off, lax.rem(me + off, n)) for off in near_first(n)]
    dp_peers = [(off, lax.rem(me_dp + off, m)) for off in near_first(m)]

    two_step = m == 4 and share % 32 == 0
    if two_step:
        low = lax.rem(me_dp, 2)
        w_peers = [(0, me_dp + 1 - 2 * low), (1, lax.rem(me_dp + 2, 4))]
    else:
        w_peers = [(at, peer) for at, (_, peer) in enumerate(dp_peers)]

    own_copies = [
        pltpu.make_async_copy(wk_ref, wf.at[me, :, pl.ds(0, HEAD_DIM)], loc_sem.at[0]),
        pltpu.make_async_copy(wv_ref, wf.at[me, :, pl.ds(HEAD_DIM, HEAD_DIM)], loc_sem.at[1]),
        pltpu.make_async_copy(tok_ref, tokf.at[head], loc_sem.at[2]),
    ]
    for copy in own_copies:
        copy.start()

    barrier = pltpu.get_barrier_semaphore()
    for _, peer in ctx_peers:
        pl.semaphore_signal(barrier, inc=1, device_id={"context": peer}, device_id_type=MESH)
    for _, peer in dp_peers:
        pl.semaphore_signal(barrier, inc=1, device_id={"dp": peer}, device_id_type=MESH)
    pl.semaphore_signal(barrier, inc=1, device_id={"head": other}, device_id_type=MESH)
    pl.semaphore_wait(barrier, n + m - 1)

    put(tok_ref, tokf.at[head], tok_sem.at[0], tok_sem.at[1], head=other)
    own_copies[0].wait()
    own_copies[1].wait()
    shared = pl.ds(pl.multiple_of(me_dp * share, 16), share)
    direct_rows = wrows - m * share
    direct = pl.ds(m * share, direct_rows)
    for off, peer in ctx_peers:
        part = wf.at[me, shared]
        put(part, part, wz_s.at[off], wz_r.at[me], context=peer)
    if direct_rows:
        for off, peer in ctx_peers:
            part = wf.at[me, direct]
            put(part, part, wd_s.at[off], wd_r.at[me], context=peer)
    own_copies[2].wait()
    arrived(tokf.at[other], tok_sem.at[0], tok_sem.at[1])

    def token_block(owner):
        column = pl.multiple_of(lax.rem(owner, half) * wrows, 128)
        return owner // half, pl.ds(column, wrows)

    def token_rows(core, part):
        start = 0 if part == 0 else early
        count = early if part == 0 else rows - early
        return pl.ds(pl.multiple_of(core * rows + start, 16), count)

    def token_copy(part, off, peer):
        span = token_rows(head, part)
        side, columns = token_block(peer)
        return copy_of(
            tokf.at[side, span, columns], tokd.at[me, span],
            td_s.at[part, off], td_r.at[part, me], context=peer,
        )

    my_side, my_columns = token_block(me)
    own_tokens = pltpu.make_async_copy(tokf.at[my_side, :, my_columns], tokd.at[me], loc_sem.at[3])
    own_tokens.start()
    for off, src in ctx_peers:
        part = wf.at[src, shared]
        arrived(part, wz_s.at[off], wz_r.at[src])
        for dp_at, peer in w_peers:
            put(part, part, wx_s.at[src, dp_at], wx_r.at[src, dp_at], dp=peer)
    if two_step:
        for off, src in ctx_peers:
            for dp_at, peer in w_peers:
                base = pl.multiple_of(peer * share, 16)
                whole = wf.at[src, pl.ds(base, share)]
                arrived(whole, wx_s.at[src, dp_at], wx_r.at[src, dp_at])
                to = w_peers[1 - dp_at][1]
                start = 0 if dp_at == 0 else share // 2
                piece = wf.at[src, pl.ds(pl.multiple_of(base + start, 16), share // 2)]
                put(piece, piece, wx_s.at[src, 2 + dp_at], wx_r.at[src, 2 + dp_at], dp=to)
    for off, peer in ctx_peers:
        copy = token_copy(0, off, peer)
        copy.start()
        sends.append((None, copy))
    for off, peer in ctx_peers:
        copy = token_copy(1, off, peer)
        pl.when(peer < me)(copy.start)
        sends.append((None, copy))

    projected = dot(tokf[my_side, :, my_columns], wf[me])
    for off, src in ctx_peers:
        if direct_rows:
            arrived(wf.at[src, direct], wd_s.at[off], wd_r.at[src])
        if two_step:
            base = (3 - me_dp) * share
            for dp_at in range(2):
                start = 0 if dp_at == 0 else share // 2
                theirs = pl.ds(pl.multiple_of(base + start, 16), share // 2)
                arrived(wf.at[src, theirs], wx_s.at[src, 2 + dp_at], wx_r.at[src, 2 + dp_at])
        else:
            for dp_at, peer in w_peers:
                origin = lax.rem(me_dp + m - dp_peers[dp_at][0], m)
                theirs = pl.ds(pl.multiple_of(origin * share, 16), share)
                arrived(wf.at[src, theirs], wx_s.at[src, dp_at], wx_r.at[src, dp_at])
        side, columns = token_block(src)
        projected += dot(tokf[side, :, columns], wf[src])
    pairs = projected.astype(jnp.bfloat16)
    my_rows = pl.ds(pl.multiple_of(me * rows, rows), rows)
    kv[my_rows, :] = pairs[:rows]
    kvn[...] = pairs[rows:]
    for off, peer in ctx_peers:
        put_if(peer > me, kv.at[my_rows], kv.at[my_rows], kv_s.at[off], kv_r.at[me], context=peer)
    put(wf.at[pl.ds(other * half, half)], wo, wo_sem.at[0], wo_sem.at[1], head=other)
    for off, peer in ctx_peers:
        pl.when(peer > me)(token_copy(1, off, peer).start)

    block = blk_ref[0]
    total_rows = n * rows
    lane = lax.broadcasted_iota(jnp.int32, (1, rows2), 1)
    noisy_lane = lane >= rows
    position = me * rows + jnp.where(noisy_lane, lane - rows, lane)
    block_start = position & (-block)
    limit = jnp.where(noisy_lane, block_start, block_start + block)
    dkv[...] = jnp.zeros_like(dkv)
    dn[...] = jnp.zeros_like(dn)
    knt[...] = kvn[:, :HEAD_DIM].T
    for off, src in ctx_peers:
        span = pl.ds(pl.multiple_of(src * rows, rows), rows)

        @pl.when(src < me)
        def _(span=span, off=off, src=src):
            arrived(kv.at[span], kv_s.at[off], kv_r.at[src])

        @pl.when(src > me)
        def _(span=span):
            kv[span, :] = jnp.zeros((rows, 2 * HEAD_DIM), jnp.bfloat16)
    kt[...] = kv[:, :HEAD_DIM].T

    def head_turn(turn, carry):
        columns = pl.ds(pl.multiple_of(turn * HEAD_DIM, HEAD_DIM), HEAD_DIM)
        q = q_ref[:, columns]
        g = g_ref[:, columns]
        keys = kv[:, :HEAD_DIM]
        values = kv[:, HEAD_DIM:]
        own_keys = kvn[:, :HEAD_DIM]
        own_values = kvn[:, HEAD_DIM:]
        key_pos = lax.broadcasted_iota(jnp.int32, (total_rows, rows2), 0)
        near = lax.broadcasted_iota(jnp.int32, (rows, rows), 0)
        same = (near ^ lax.broadcasted_iota(jnp.int32, (rows, rows), 1)) < block
        s = jnp.where(key_pos < limit, dot_nt(keys, q) * score_scale, MASKED)
        s_own = jnp.where(same, dot_nt(own_keys, q[rows:]) * score_scale, MASKED)
        peak = jnp.max(s, axis=0, keepdims=True)
        peak_own = jnp.maximum(peak[:, rows:], jnp.max(s_own, axis=0, keepdims=True))
        peak = jnp.concatenate([peak[:, :rows], peak_own], axis=1)
        e = jnp.exp(s - peak)
        e_own = jnp.exp(s_own - peak_own)
        total = jnp.sum(e, axis=0, keepdims=True)
        total_own = total[:, rows:] + jnp.sum(e_own, axis=0, keepdims=True)
        inverse = 1.0 / jnp.concatenate([total[:, :rows], total_own], axis=1)
        p = e * inverse
        p_own = e_own * inverse[:, rows:]
        p_half = p.astype(jnp.bfloat16)
        p_half_own = p_own.astype(jnp.bfloat16)
        gp = dot_nt(values, g)
        gp_own = dot_nt(own_values, g[rows:])
        delta = jnp.sum(p_half.astype(jnp.float32) * gp, axis=0, keepdims=True)
        delta_own = delta[:, rows:] + jnp.sum(
            p_half_own.astype(jnp.float32) * gp_own, axis=0, keepdims=True
        )
        delta = jnp.concatenate([delta[:, :rows], delta_own], axis=1)
        ds = (p * (gp - delta)).astype(jnp.bfloat16)
        ds_own = (p_own * (gp_own - delta_own)).astype(jnp.bfloat16)
        dkv[:, :HEAD_DIM] += dot(ds, q)
        dkv[:, HEAD_DIM:] += dot(p_half, g)
        dn[:, :HEAD_DIM] += dot(ds_own, q[rows:])
        dn[:, HEAD_DIM:] += dot(p_half_own, g[rows:])
        dq = dot(kt[...], ds)
        dq_own = dq[:, rows:] + dot(knt[...], ds_own)
        dq_ref[:rows, columns] = (dq[:, :rows] * score_scale).T.astype(jnp.bfloat16)
        dq_ref[rows:, columns] = (dq_own * score_scale).T.astype(jnp.bfloat16)
        return carry

    lax.fori_loop(0, q_ref.shape[1] // HEAD_DIM, head_turn, 0)

    pair_scale = jnp.where(
        lax.broadcasted_iota(jnp.int32, (1, 2 * HEAD_DIM), 1) < HEAD_DIM, score_scale, 1.0
    )
    for block_at in range(n):
        pgp[block_at] = (dkv[block_at * rows : (block_at + 1) * rows] * pair_scale).astype(jnp.bfloat16)
    clean, noisy = pl.ds(0, rows), pl.ds(rows, rows)
    for off, peer in ctx_peers:
        put_if(peer < me, pgp.at[peer], pin.at[me], pp_s.at[off], pp_r.at[me], context=peer)
    pga[me, noisy] = (dn[...] * pair_scale).astype(jnp.bfloat16)
    part = pga.at[me, noisy]
    put(part, pgo.at[noisy], po_sem.at[0], po_sem.at[1], head=other)
    for off, peer in ctx_peers:
        put(part, part, pn_s.at[off], pn_r.at[me], context=peer)
    dkv[my_rows, :] *= pair_scale
    for off, src in ctx_peers:

        @pl.when(src > me)
        def _(off=off, src=src):
            arrived(pin.at[src], pp_s.at[off], pp_r.at[src])
            dkv[my_rows, :] += pin[src].astype(jnp.float32)

    pga[me, clean] = dkv[my_rows, :].astype(jnp.bfloat16)
    part = pga.at[me, clean]
    for off, peer in ctx_peers:
        put(part, part, pc_s.at[off], pc_r.at[me], context=peer)
    put(part, pgo.at[clean], po_sem.at[2], po_sem.at[3], head=other)

    for off, src in ctx_peers:
        for piece in range(2):
            span = token_rows(head, piece)
            part = tokd.at[src, span]
            arrived(part, td_s.at[piece, off], td_r.at[piece, src])
            put(part, part, tf_s.at[piece, off], tf_r.at[piece, src], head=other)
    own_tokens.wait()
    arrived(wo, wo_sem.at[0], wo_sem.at[1])
    arrived(pgo.at[noisy], po_sem.at[0], po_sem.at[1])
    arrived(pgo.at[clean], po_sem.at[2], po_sem.at[3])

    for at in range(half):
        gx_ref[:, at * wrows : (at + 1) * wrows] = (
            dot_nt(pga[me], wf[head * half + at]) + dot_nt(pgo[...], wo[at])
        ).astype(jnp.bfloat16)

    gw = dot(pga[me].T, tokd[me])
    for off, src in ctx_peers:
        for piece in range(2):
            span = token_rows(other, piece)
            arrived(tokd.at[src, span], tf_s.at[piece, off], tf_r.at[piece, src])
        arrived(pga.at[src, noisy], pn_s.at[off], pn_r.at[src])
        arrived(pga.at[src, clean], pc_s.at[off], pc_r.at[src])
        gw += dot(pga[src].T, tokd[src])

    slab = gw.shape[0] // m
    for at in range(m):
        gsum[at] = gw[at * slab : (at + 1) * slab]
        rp[at] = gw[at * slab : (at + 1) * slab].astype(jnp.bfloat16)
    for off, peer in dp_peers:
        put(rp.at[peer], rin.at[me_dp], rs_s.at[off], rs_r.at[me_dp], dp=peer)
    slab_sum = gsum[me_dp]
    for off, src in dp_peers:
        arrived(rin.at[src], rs_s.at[off], rs_r.at[src])
        slab_sum += rin[src].astype(jnp.float32)
    rall[me_dp] = slab_sum.astype(jnp.bfloat16)
    for off, peer in dp_peers:
        put(rall.at[me_dp], rall.at[me_dp], ra_s.at[off], ra_r.at[me_dp], dp=peer)
    for off, src in dp_peers:
        arrived(rall.at[src], ra_s.at[off], ra_r.at[src])
    for at in range(m):
        gsum[at] = rall[at].astype(jnp.float32)
    gwk_ref[...] = gsum[: m // 2].reshape(HEAD_DIM, wrows).T
    gwv_ref[...] = gsum[m // 2 :].reshape(HEAD_DIM, wrows).T
    for condition, copy in sends:
        if condition is None:
            copy.wait_send()
        else:
            pl.when(condition)(copy.wait_send)


def per_device(tokens, queries, grad_out, w_key, w_value, block_len):
    n = lax.axis_size("context")
    m = lax.axis_size("dp")
    rows = tokens.shape[2]
    features = tokens.shape[3]
    wrows, width = w_key.shape
    q_width = queries.shape[3]
    share = wrows // m // 16 * 16
    early = max(16, rows // 64 * 16)
    half = n // 2
    pair = 2 * width
    bf16, f32 = jnp.bfloat16, jnp.float32
    vmem = pl.BlockSpec(memory_space=pltpu.VMEM)
    dma = pltpu.SemaphoreType.DMA
    slab = pair // m
    dq, gx, gwk, gwv = pl.pallas_call(
        functools.partial(fused_kernel, n, m, share, early),
        out_shape=(
            jax.ShapeDtypeStruct((2 * rows, q_width), bf16),
            jax.ShapeDtypeStruct((2 * rows, features), bf16),
            jax.ShapeDtypeStruct((wrows, width), f32),
            jax.ShapeDtypeStruct((wrows, width), f32),
        ),
        in_specs=[pl.BlockSpec(memory_space=pltpu.SMEM)] + [vmem] * 5,
        out_specs=(vmem, vmem, vmem, vmem),
        scratch_shapes=[
            pltpu.VMEM((2, 2 * rows, features), bf16),
            pltpu.VMEM((n, wrows, pair), bf16),
            pltpu.VMEM((half, wrows, pair), bf16),
            pltpu.VMEM((n * rows, pair), bf16),
            pltpu.VMEM((rows, pair), bf16),
            pltpu.VMEM((width, n * rows), bf16),
            pltpu.VMEM((width, rows), bf16),
            pltpu.VMEM((n * rows, pair), f32),
            pltpu.VMEM((rows, pair), f32),
            pltpu.VMEM((n, rows, pair), bf16),
            pltpu.VMEM((n, rows, pair), bf16),
            pltpu.VMEM((n, 2 * rows, pair), bf16),
            pltpu.VMEM((2 * rows, pair), bf16),
            pltpu.VMEM((n, 2 * rows, wrows), bf16),
            pltpu.VMEM((m, slab, wrows), f32),
            pltpu.VMEM((m, slab, wrows), bf16),
            pltpu.VMEM((m, slab, wrows), bf16),
            pltpu.VMEM((m, slab, wrows), bf16),
            dma((4,)), dma((2,)), dma((n,)), dma((n,)), dma((n,)), dma((n,)),
            dma((n, m)), dma((n, m)), dma((2,)), dma((n,)), dma((n,)),
            dma((2, n)), dma((2, n)), dma((2, n)), dma((2, n)),
            dma((n,)), dma((n,)), dma((n,)), dma((n,)), dma((n,)), dma((n,)),
            dma((4,)), dma((m,)), dma((m,)), dma((m,)), dma((m,)),
        ],
        compiler_params=pltpu.CompilerParams(
            collective_id=0, has_side_effects=True, vmem_limit_bytes=60 * 1024 * 1024
        ),
    )(
        block_len,
        tokens.reshape(2 * rows, features),
        queries.reshape(2 * rows, q_width),
        grad_out.reshape(2 * rows, q_width),
        w_key,
        w_value,
    )
    return (
        dq.reshape(queries.shape),
        gx.reshape(tokens.shape),
        gwk,
        gwv,
    )


def solution(mesh):
    placed = (
        P("dp", None, "context", "head"),
        P("dp", None, "context", "head"),
        P("dp", None, "context", "head"),
        P("context", "head"),
        P("context", "head"),
        P("dp"),
    )
    return jax.shard_map(
        per_device,
        mesh=mesh,
        in_specs=placed,
        out_specs=(
            P("dp", None, "context", "head"),
            P("dp", None, "context", "head"),
            P("context", "head"),
            P("context", "head"),
        ),
        check_vma=False,
    )
```

profile of v0, /device:TPU:0, one launch (start us, length us, event | category | flops | bytes accessed | tf_op | source)
XLA Modules:
  0.0 85.7 jit_solution(9605043799375072434)
XLA Ops:
  1.3 79.0 %shard_map.93 = (bf16[256,1024]{1,0:T(8,128)(2,1)}, bf16[256,2048]{1,0:T(8,128)(2,1)}, f32[1024,128]{1,0:T(8,128)}, f32[1024,128]{1,0:T(8,128)}) custom-call(s32[1]{0:T(128)S(6)} %copy.14.blk_ref, bf16[256,2048]{1,0:T(8,128)(2,1)} %bitcast.5, bf16[256,1024]{1,0:T(8,128)(2,1)} %bitcast.8, bf16[256,1024]{1,0:T(8,128)(2,1)} %bitcast.9, ...), custom_call_target="tpu_custom_call" | custom-call | tf_op jit(solution)/shard_map/pallas_call | solution.py:346
  80.3 0.0 copy-start
  80.3 2.0 %copy.15 = bf16[1,2,128,1024]{3,2,1,0:T(8,128)(2,1)} copy(bf16[1,2,128,1024]{3,2,1,0:T(8,128)(2,1)} %bitcast.7) | data formatting | bytes 1048576
  82.3 0.0 copy-done
  82.3 0.0 copy-start.2
  82.3 1.0 %copy.16 = bf16[1,2,128,2048]{3,2,1,0:T(8,128)(2,1)} copy(bf16[1,2,128,2048]{3,2,1,0:T(8,128)(2,1)S(1)} %bitcast.6) | data formatting | bytes 2097152
  83.3 0.4 copy-done.2
  83.7 0.0 copy-start.1
  83.7 0.8 copy.17
  84.5 0.4 copy-done.1
  84.9 0.8 copy.18
Async XLA Ops:
  80.3 2.0 %copy-start = (bf16[256,2048]{1,0:T(8,128)(2,1)S(1)}, bf16[256,2048]{1,0:T(8,128)(2,1)}, u32[]{:S(2)}) copy-start(bf16[256,2048]{1,0:T(8,128)(2,1)} %get-tuple-element.9) | copy-start | bytes 3145732
  82.3 1.4 %copy-start.2 = (f32[1024,128]{1,0:T(8,128)S(1)}, f32[1024,128]{1,0:T(8,128)}, u32[]{:S(2)}) copy-start(f32[1024,128]{1,0:T(8,128)} %get-tuple-element.18) | copy-start | bytes 1572868
  83.7 1.2 %copy-start.1 = (f32[1024,128]{1,0:T(8,128)S(1)}, f32[1024,128]{1,0:T(8,128)}, u32[]{:S(2)}) copy-start(f32[1024,128]{1,0:T(8,128)} %get-tuple-element.19) | copy-start | bytes 1572868
where the time goes:
time: 86.5 us; the launch traced here: 85.7 us
  Pallas kernels  79 us (91%)
  local copies, waits for them, and re-layouts  5.38 us (6%)
  between operations  1.3 us (2%)
    pallas_call x1, Pallas kernels, per_device(): pl.pallas_call(functools.partial(fused_kernel, n, m, share, early), out_s...  79 us
    unnamed x10, local copies, waits for them, and re-layouts  5.38 us

commit v1 on v0

--- a/solution.py
+++ b/solution.py
@@ -10,6 +10,7 @@
 
 HEAD_DIM = 128
 MASKED = -1e30
+VMEM_LIMIT = 56 * 1024 * 1024
 MESH = pl.DeviceIdType.MESH
 NT = (((1,), (1,)), ((), ()))
 
@@ -23,6 +24,18 @@
     return order
 
 
+def line_order(me, n):
+    low, high = me, n - 1 - me
+    both = jnp.minimum(low, high)
+    longer = jnp.where(low < high, 1, -1)
+    order = []
+    for k in range(1, n):
+        near_side = 1 if k % 2 else -1
+        peer = jnp.where(k <= 2 * both, me + near_side * ((k + 1) // 2), me + longer * (k - both))
+        order.append((k, peer))
+    return order
+
+
 def dot(left, right):
     return jnp.dot(left, right, preferred_element_type=jnp.float32)
 
@@ -33,9 +46,9 @@
 
 def fused_kernel(
     n, m, share, early,
-    blk_ref, tok_ref, q_ref, g_ref, wk_ref, wv_ref,
+    blk_ref, tok_ref, qin_ref, gin_ref, wk_ref, wv_ref,
     dq_ref, gx_ref, gwk_ref, gwv_ref,
-    tokf, wf, wo, kv, kvn, kt, knt, dkv, dn, pgp, pin, pga, pgo, tokd, gsum, rp, rin, rall,
+    q_ref, g_ref, tokf, wf, wo, kv, kvn, kt, knt, dkv, dn, pgp, pin, pga, pgo, tokd, gsum, rp, rin, rall,
     loc_sem, tok_sem, wz_s, wz_r, wd_s, wd_r, wx_s, wx_r, wo_sem, kv_s, kv_r,
     td_s, td_r, tf_s, tf_r, pp_s, pp_r, pn_s, pn_r, pc_s, pc_r, po_sem, rs_s, rs_r, ra_s, ra_r,
 ):
@@ -69,7 +82,8 @@
     def arrived(dst, send_sem, recv_sem):
         copy_of(dst, dst, send_sem, recv_sem, head=other).wait_recv()
 
-    ctx_peers = [(off, lax.rem(me + off, n)) for off in near_first(n)]
+    near = line_order(me, n)
+    far = near[::-1]
     dp_peers = [(off, lax.rem(me_dp + off, m)) for off in near_first(m)]
 
     two_step = m == 4 and share % 32 == 0
@@ -83,33 +97,45 @@
         pltpu.make_async_copy(wk_ref, wf.at[me, :, pl.ds(0, HEAD_DIM)], loc_sem.at[0]),
         pltpu.make_async_copy(wv_ref, wf.at[me, :, pl.ds(HEAD_DIM, HEAD_DIM)], loc_sem.at[1]),
         pltpu.make_async_copy(tok_ref, tokf.at[head], loc_sem.at[2]),
+        pltpu.make_async_copy(qin_ref, q_ref, loc_sem.at[4]),
+        pltpu.make_async_copy(gin_ref, g_ref, loc_sem.at[5]),
     ]
     for copy in own_copies:
         copy.start()
 
     barrier = pltpu.get_barrier_semaphore()
-    for _, peer in ctx_peers:
+    for _, peer in near:
         pl.semaphore_signal(barrier, inc=1, device_id={"context": peer}, device_id_type=MESH)
     for _, peer in dp_peers:
         pl.semaphore_signal(barrier, inc=1, device_id={"dp": peer}, device_id_type=MESH)
     pl.semaphore_signal(barrier, inc=1, device_id={"head": other}, device_id_type=MESH)
     pl.semaphore_wait(barrier, n + m - 1)
 
-    put(tok_ref, tokf.at[head], tok_sem.at[0], tok_sem.at[1], head=other)
+    shared_base = pl.multiple_of(me_dp * share, 16)
+    chunks = 2 if two_step else 1
+    piece_rows = share // chunks
+
+    def w_piece(owner, base, chunk):
+        return wf.at[owner, pl.ds(pl.multiple_of(base + chunk * piece_rows, 16), piece_rows)]
+
+    direct_rows = wrows - m * share
+    direct = pl.ds(m * share, direct_rows)
     own_copies[0].wait()
     own_copies[1].wait()
-    shared = pl.ds(pl.multiple_of(me_dp * share, 16), share)
-    direct_rows = wrows - m * share
-    direct = pl.ds(m * share, direct_rows)
-    for off, peer in ctx_peers:
-        part = wf.at[me, shared]
-        put(part, part, wz_s.at[off], wz_r.at[me], context=peer)
+    for chunk in range(chunks):
+        part = w_piece(me, shared_base, chunk)
+        for side in (1, -1):
+            peer = me + side
+            put_if(
+                (peer >= 0) & (peer < n), part, part,
+                wz_s.at[0, chunk, (side + 1) // 2], wz_r.at[me, chunk], context=peer,
+            )
+    own_copies[2].wait()
+    put(tokf.at[head], tokf.at[head], tok_sem.at[0], tok_sem.at[1], head=other)
     if direct_rows:
-        for off, peer in ctx_peers:
+        for k, peer in near:
             part = wf.at[me, direct]
-            put(part, part, wd_s.at[off], wd_r.at[me], context=peer)
-    own_copies[2].wait()
-    arrived(tokf.at[other], tok_sem.at[0], tok_sem.at[1])
+            put(part, part, wd_s.at[k], wd_r.at[me], context=peer)
 
     def token_block(owner):
         column = pl.multiple_of(lax.rem(owner, half) * wrows, 128)
@@ -129,58 +155,65 @@
         )
 
     my_side, my_columns = token_block(me)
+    def w_forward(src):
+        for dp_at, peer in w_peers:
+            base = peer * share
+            part = w_piece(src, base, dp_at)
+            arrived(part, wx_s.at[src, dp_at, dp_at], wx_r.at[src, dp_at, dp_at])
+            to = w_peers[1 - dp_at][1]
+            put(part, part, wx_s.at[src, 2, dp_at], wx_r.at[src, 2, dp_at], dp=to)
+
+    for k, src in near:
+        onward = jnp.where(src > me, me - 1, me + 1)
+        for chunk in range(chunks):
+            part = w_piece(src, shared_base, chunk)
+            arrived(part, wz_s.at[k, chunk, 0], wz_r.at[src, chunk])
+            put_if(
+                (onward >= 0) & (onward < n), part, part,
+                wz_s.at[k, chunk, 0], wz_r.at[src, chunk], context=onward,
+            )
+            for dp_at, peer in w_peers:
+                put(part, part, wx_s.at[src, dp_at, chunk], wx_r.at[src, dp_at, chunk], dp=peer)
+        if two_step and k > 1:
+            w_forward(near[k - 2][1])
+    arrived(tokf.at[other], tok_sem.at[0], tok_sem.at[1])
+    for k, peer in far:
+        copy = token_copy(0, k, peer)
+        copy.start()
+        sends.append((None, copy))
+    for k, peer in far:
+        copy = token_copy(1, k, peer)
+        pl.when(peer < me)(copy.start)
+        sends.append((None, copy))
     own_tokens = pltpu.make_async_copy(tokf.at[my_side, :, my_columns], tokd.at[me], loc_sem.at[3])
     own_tokens.start()
-    for off, src in ctx_peers:
-        part = wf.at[src, shared]
-        arrived(part, wz_s.at[off], wz_r.at[src])
-        for dp_at, peer in w_peers:
-            put(part, part, wx_s.at[src, dp_at], wx_r.at[src, dp_at], dp=peer)
     if two_step:
-        for off, src in ctx_peers:
+        w_forward(near[-1][1])
+
+    projected = dot(tokf[my_side, :, my_columns], wf[me])
+    for k, src in near:
+        if direct_rows:
+            arrived(wf.at[src, direct], wd_s.at[k], wd_r.at[src])
+        if two_step:
             for dp_at, peer in w_peers:
-                base = pl.multiple_of(peer * share, 16)
-                whole = wf.at[src, pl.ds(base, share)]
-                arrived(whole, wx_s.at[src, dp_at], wx_r.at[src, dp_at])
-                to = w_peers[1 - dp_at][1]
-                start = 0 if dp_at == 0 else share // 2
-                piece = wf.at[src, pl.ds(pl.multiple_of(base + start, 16), share // 2)]
-                put(piece, piece, wx_s.at[src, 2 + dp_at], wx_r.at[src, 2 + dp_at], dp=to)
-    for off, peer in ctx_peers:
-        copy = token_copy(0, off, peer)
-        copy.start()
-        sends.append((None, copy))
-    for off, peer in ctx_peers:
-        copy = token_copy(1, off, peer)
-        pl.when(peer < me)(copy.start)
-        sends.append((None, copy))
-
-    projected = dot(tokf[my_side, :, my_columns], wf[me])
-    for off, src in ctx_peers:
-        if direct_rows:
-            arrived(wf.at[src, direct], wd_s.at[off], wd_r.at[src])
-        if two_step:
-            base = (3 - me_dp) * share
-            for dp_at in range(2):
-                start = 0 if dp_at == 0 else share // 2
-                theirs = pl.ds(pl.multiple_of(base + start, 16), share // 2)
-                arrived(wf.at[src, theirs], wx_s.at[src, 2 + dp_at], wx_r.at[src, 2 + dp_at])
+                part = w_piece(src, peer * share, 1 - dp_at)
+                arrived(part, wx_s.at[src, dp_at, 1 - dp_at], wx_r.at[src, dp_at, 1 - dp_at])
+                part = w_piece(src, (3 - me_dp) * share, dp_at)
+                arrived(part, wx_s.at[src, 2, dp_at], wx_r.at[src, 2, dp_at])
         else:
             for dp_at, peer in w_peers:
                 origin = lax.rem(me_dp + m - dp_peers[dp_at][0], m)
-                theirs = pl.ds(pl.multiple_of(origin * share, 16), share)
-                arrived(wf.at[src, theirs], wx_s.at[src, dp_at], wx_r.at[src, dp_at])
+                part = w_piece(src, origin * share, 0)
+                arrived(part, wx_s.at[src, dp_at, 0], wx_r.at[src, dp_at, 0])
         side, columns = token_block(src)
         projected += dot(tokf[side, :, columns], wf[src])
     pairs = projected.astype(jnp.bfloat16)
     my_rows = pl.ds(pl.multiple_of(me * rows, rows), rows)
     kv[my_rows, :] = pairs[:rows]
     kvn[...] = pairs[rows:]
-    for off, peer in ctx_peers:
-        put_if(peer > me, kv.at[my_rows], kv.at[my_rows], kv_s.at[off], kv_r.at[me], context=peer)
+    for k, peer in far:
+        put_if(peer > me, kv.at[my_rows], kv.at[my_rows], kv_s.at[k], kv_r.at[me], context=peer)
     put(wf.at[pl.ds(other * half, half)], wo, wo_sem.at[0], wo_sem.at[1], head=other)
-    for off, peer in ctx_peers:
-        pl.when(peer > me)(token_copy(1, off, peer).start)
 
     block = blk_ref[0]
     total_rows = n * rows
@@ -192,16 +225,20 @@
     dkv[...] = jnp.zeros_like(dkv)
     dn[...] = jnp.zeros_like(dn)
     knt[...] = kvn[:, :HEAD_DIM].T
-    for off, src in ctx_peers:
+    own_copies[3].wait()
+    own_copies[4].wait()
+    for k, src in near:
         span = pl.ds(pl.multiple_of(src * rows, rows), rows)
 
         @pl.when(src < me)
-        def _(span=span, off=off, src=src):
-            arrived(kv.at[span], kv_s.at[off], kv_r.at[src])
+        def _(span=span, k=k, src=src):
+            arrived(kv.at[span], kv_s.at[k], kv_r.at[src])
 
         @pl.when(src > me)
         def _(span=span):
             kv[span, :] = jnp.zeros((rows, 2 * HEAD_DIM), jnp.bfloat16)
+    for k, peer in far:
+        pl.when(peer > me)(token_copy(1, k, peer).start)
     kt[...] = kv[:, :HEAD_DIM].T
 
     def head_turn(turn, carry):
@@ -256,33 +293,55 @@
     for block_at in range(n):
         pgp[block_at] = (dkv[block_at * rows : (block_at + 1) * rows] * pair_scale).astype(jnp.bfloat16)
     clean, noisy = pl.ds(0, rows), pl.ds(rows, rows)
-    for off, peer in ctx_peers:
-        put_if(peer < me, pgp.at[peer], pin.at[me], pp_s.at[off], pp_r.at[me], context=peer)
+    for k, peer in far:
+        put_if(peer < me, pgp.at[peer], pin.at[me], pp_s.at[k], pp_r.at[me], context=peer)
     pga[me, noisy] = (dn[...] * pair_scale).astype(jnp.bfloat16)
     part = pga.at[me, noisy]
+
+    def noisy_copy(k, peer):
+        return copy_of(part, part, pn_s.at[k], pn_r.at[me], context=peer)
+
+    for k, peer in far:
+        copy = noisy_copy(k, peer)
+        pl.when(peer > me)(copy.start)
+        sends.append((None, copy))
     put(part, pgo.at[noisy], po_sem.at[0], po_sem.at[1], head=other)
-    for off, peer in ctx_peers:
-        put(part, part, pn_s.at[off], pn_r.at[me], context=peer)
     dkv[my_rows, :] *= pair_scale
-    for off, src in ctx_peers:
+
+    def token_onward(k, src, piece):
+        span = token_rows(head, piece)
+        held = tokd.at[src, span]
+        arrived(held, td_s.at[piece, k], td_r.at[piece, src])
+        copy = copy_of(held, held, tf_s.at[piece, k], tf_r.at[piece, src], head=other)
+        copy.start()
+
+    for k, src in near:
+        token_onward(k, src, 0)
+        sends.append((None, copy_of(
+            tokd.at[src, token_rows(head, 0)], tokd.at[src, token_rows(head, 0)],
+            tf_s.at[0, k], tf_r.at[0, src], head=other,
+        )))
+    for k, src in near:
 
         @pl.when(src > me)
-        def _(off=off, src=src):
-            arrived(pin.at[src], pp_s.at[off], pp_r.at[src])
+        def _(k=k, src=src):
+            arrived(pin.at[src], pp_s.at[k], pp_r.at[src])
             dkv[my_rows, :] += pin[src].astype(jnp.float32)
 
     pga[me, clean] = dkv[my_rows, :].astype(jnp.bfloat16)
-    part = pga.at[me, clean]
-    for off, peer in ctx_peers:
-        put(part, part, pc_s.at[off], pc_r.at[me], context=peer)
-    put(part, pgo.at[clean], po_sem.at[2], po_sem.at[3], head=other)
-
-    for off, src in ctx_peers:
-        for piece in range(2):
-            span = token_rows(head, piece)
-            part = tokd.at[src, span]
-            arrived(part, td_s.at[piece, off], td_r.at[piece, src])
-            put(part, part, tf_s.at[piece, off], tf_r.at[piece, src], head=other)
+    whole = pga.at[me, clean]
+    for k, peer in far:
+        put(whole, whole, pc_s.at[k], pc_r.at[me], context=peer)
+    for k, peer in far:
+        pl.when(peer < me)(noisy_copy(k, peer).start)
+    put(whole, pgo.at[clean], po_sem.at[2], po_sem.at[3], head=other)
+
+    for k, src in near:
+        token_onward(k, src, 1)
+        sends.append((None, copy_of(
+            tokd.at[src, token_rows(head, 1)], tokd.at[src, token_rows(head, 1)],
+            tf_s.at[1, k], tf_r.at[1, src], head=other,
+        )))
     own_tokens.wait()
     arrived(wo, wo_sem.at[0], wo_sem.at[1])
     arrived(pgo.at[noisy], po_sem.at[0], po_sem.at[1])
@@ -294,12 +353,12 @@
         ).astype(jnp.bfloat16)
 
     gw = dot(pga[me].T, tokd[me])
-    for off, src in ctx_peers:
+    for k, src in near:
         for piece in range(2):
             span = token_rows(other, piece)
-            arrived(tokd.at[src, span], tf_s.at[piece, off], tf_r.at[piece, src])
-        arrived(pga.at[src, noisy], pn_s.at[off], pn_r.at[src])
-        arrived(pga.at[src, clean], pc_s.at[off], pc_r.at[src])
+            arrived(tokd.at[src, span], tf_s.at[piece, k], tf_r.at[piece, src])
+        arrived(pga.at[src, noisy], pn_s.at[k], pn_r.at[src])
+        arrived(pga.at[src, clean], pc_s.at[k], pc_r.at[src])
         gw += dot(pga[src].T, tokd[src])
 
     slab = gw.shape[0] // m
@@ -328,6 +387,15 @@
             pl.when(condition)(copy.wait_send)
 
 
+def store_kernel(dq_in, gx_in, gwk_in, gwv_in, dq_out, gx_out, gwk_out, gwv_out, sem):
+    pairs = ((gx_in, gx_out), (dq_in, dq_out), (gwk_in, gwk_out), (gwv_in, gwv_out))
+    copies = [pltpu.make_async_copy(src, dst, sem.at[at]) for at, (src, dst) in enumerate(pairs)]
+    for copy in copies:
+        copy.start()
+    for copy in copies:
+        copy.wait()
+
+
 def per_device(tokens, queries, grad_out, w_key, w_value, block_len):
     n = lax.axis_size("context")
     m = lax.axis_size("dp")
@@ -342,18 +410,22 @@
     bf16, f32 = jnp.bfloat16, jnp.float32
     vmem = pl.BlockSpec(memory_space=pltpu.VMEM)
     dma = pltpu.SemaphoreType.DMA
+    hbm = pl.BlockSpec(memory_space=pltpu.HBM)
     slab = pair // m
+    results = (
+        ((2 * rows, q_width), bf16),
+        ((2 * rows, features), bf16),
+        ((wrows, width), f32),
+        ((wrows, width), f32),
+    )
     dq, gx, gwk, gwv = pl.pallas_call(
         functools.partial(fused_kernel, n, m, share, early),
-        out_shape=(
-            jax.ShapeDtypeStruct((2 * rows, q_width), bf16),
-            jax.ShapeDtypeStruct((2 * rows, features), bf16),
-            jax.ShapeDtypeStruct((wrows, width), f32),
-            jax.ShapeDtypeStruct((wrows, width), f32),
-        ),
-        in_specs=[pl.BlockSpec(memory_space=pltpu.SMEM)] + [vmem] * 5,
+        out_shape=tuple(pltpu.VMEM(*result) for result in results),
+        in_specs=[pl.BlockSpec(memory_space=pltpu.SMEM)] + [hbm] * 5,
         out_specs=(vmem, vmem, vmem, vmem),
         scratch_shapes=[
+            pltpu.VMEM((2 * rows, q_width), bf16),
+            pltpu.VMEM((2 * rows, q_width), bf16),
             pltpu.VMEM((2, 2 * rows, features), bf16),
             pltpu.VMEM((n, wrows, pair), bf16),
             pltpu.VMEM((half, wrows, pair), bf16),
@@ -372,14 +444,14 @@
             pltpu.VMEM((m, slab, wrows), bf16),
             pltpu.VMEM((m, slab, wrows), bf16),
             pltpu.VMEM((m, slab, wrows), bf16),
-            dma((4,)), dma((2,)), dma((n,)), dma((n,)), dma((n,)), dma((n,)),
-            dma((n, m)), dma((n, m)), dma((2,)), dma((n,)), dma((n,)),
+            dma((6,)), dma((2,)), dma((n, 2, 2)), dma((n, 2)), dma((n,)), dma((n,)),
+            dma((n, m, 2)), dma((n, m, 2)), dma((2,)), dma((n,)), dma((n,)),
             dma((2, n)), dma((2, n)), dma((2, n)), dma((2, n)),
             dma((n,)), dma((n,)), dma((n,)), dma((n,)), dma((n,)), dma((n,)),
             dma((4,)), dma((m,)), dma((m,)), dma((m,)), dma((m,)),
         ],
         compiler_params=pltpu.CompilerParams(
-            collective_id=0, has_side_effects=True, vmem_limit_bytes=60 * 1024 * 1024
+            collective_id=0, has_side_effects=True, vmem_limit_bytes=VMEM_LIMIT
         ),
     )(
         block_len,
@@ -389,6 +461,13 @@
         w_key,
         w_value,
     )
+    dq, gx, gwk, gwv = pl.pallas_call(
+        store_kernel,
+        out_shape=tuple(jax.ShapeDtypeStruct(*result) for result in results),
+        in_specs=[vmem] * 4,
+        out_specs=(hbm, hbm, hbm, hbm),
+        scratch_shapes=[dma((4,))],
+    )(*(pltpu.with_memory_space_constraint(x, pltpu.VMEM) for x in (dq, gx, gwk, gwv)))
     return (
         dq.reshape(queries.shape),
         gx.reshape(tokens.shape),

time: 86.5 us -> 76.4 us (0.88)
  local copies, waits for them, and re-layouts: 5.38 us -> 0 us
  Pallas kernels: 79 us -> 75 us
    pallas_call x1, Pallas kernels: 79 us -> 73.5 us  [per_device(): pl.pallas_call(functools.partial(fused_kernel, n, m, share, early), out_s...]
    unnamed x10 -> x0, local copies, waits for them, and re-layouts: 5.38 us -> none
    pallas_call x0 -> x1, Pallas kernels: none -> 1.52 us  [per_device(): pl.pallas_call(store_kernel, out_shape=tuple((jax.ShapeDtypeStruct(*resul...]
where the time goes in v1:
time: 76.4 us; the launch traced here: 76.3 us
  Pallas kernels  75 us (98%)
  between operations  1.29 us (2%)
    pallas_call x1, Pallas kernels, per_device(): pl.pallas_call(functools.partial(fused_kernel, n, m, share, early), out_s...  73.5 us

profile of v1, /device:TPU:0, one launch (start us, length us, event | category | flops | bytes accessed | tf_op | source)
XLA Modules:
  0.0 76.3 jit_solution(10837964865191128667)
XLA Ops:
  1.3 73.5 %shard_map.93 = (bf16[256,1024]{1,0:T(8,128)(2,1)S(1)}, bf16[256,2048]{1,0:T(8,128)(2,1)S(1)}, f32[1024,128]{1,0:T(8,128)S(1)}, f32[1024,128]{1,0:T(8,128)S(1)}) custom-call(s32[1]{0:T(128)S(6)} %copy.10.blk_ref, bf16[256,2048]{1,0:T(8,128)(2,1)} %bitcast.5, bf16[256,1024]{1,0:T(8,128)(2,1)} %bitcast.6, bf16[256,1024]{1,0:T(8,128)(2,1)} %bitcast.7, ...), custom_call_target="tpu_custom_call" | custom-call | tf_op jit(solution)/shard_map/pallas_call | solution.py:421
  74.7 1.5 %shard_map.94 = (bf16[256,1024]{1,0:T(8,128)(2,1)}, bf16[256,2048]{1,0:T(8,128)(2,1)}, f32[1024,128]{1,0:T(8,128)}, f32[1024,128]{1,0:T(8,128)}) custom-call(bf16[256,1024]{1,0:T(8,128)(2,1)S(1)} %get-tuple-element.12.dq_in, bf16[256,2048]{1,0:T(8,128)(2,1)S(1)} %get-tuple-element.13.gx_in, f32[1024,128]{1,0:T(8,128)S(1)} %get-tuple-element.14.gwk_in, ...), custom_call_target="tpu_custom_call" | custom-call | tf_op jit(solution)/shard_map/pallas_call | solution.py:464

commit v2 on v1

v2 whole, which is shorter than its diff:
```python
import functools
import math

import jax
import jax.numpy as jnp
from jax import lax
from jax.experimental import pallas as pl
from jax.experimental.pallas import tpu as pltpu
from jax.sharding import PartitionSpec as P

HEAD_DIM = 128
MASKED = -1e30
VMEM_LIMIT = 56 * 1024 * 1024
MESH = pl.DeviceIdType.MESH
NT = (((1,), (1,)), ((), ()))


def line_order(me, n):
    low, high = me, n - 1 - me
    both = jnp.minimum(low, high)
    longer = jnp.where(low < high, 1, -1)
    order = []
    for k in range(1, n):
        near_side = 1 if k % 2 else -1
        peer = jnp.where(k <= 2 * both, me + near_side * ((k + 1) // 2), me + longer * (k - both))
        order.append((k, peer))
    return order


def dot(left, right):
    return jnp.dot(left, right, preferred_element_type=jnp.float32)


def dot_nt(left, right):
    return lax.dot_general(left, right, NT, preferred_element_type=jnp.float32)


def fused_kernel(
    n, m, share,
    blk_ref, tok_ref, q_in, g_in, wk_ref, wv_ref,
    dq_ref, gx_ref, gwk_ref, gwv_ref,
    qg, tokf, wf, wo, kv, kvn, kt, knt, dkv, dn, pgp, pin, pga, pgo, tokd, tokn,
    gsum, rp, rin, rall, fp, fin, foreign_own, zout, zin,
    loc_sem, pair_sem, kv_credit, pin_credit, tok_sem, wz_s, wz_r, wd_s, wd_r, wx_s, wx_r, wo_sem, kv_s, kv_r,
    t1_s, t1_r, f1_s, f1_r, t2_s, t2_r, f2_s, f2_r, pp_s, pp_r, pg_s, pn_r, pc_r, po_sem,
    rf_s, rf_r, z_sem, rs_s, rs_r, ra_s, ra_r,
):
    me_dp = lax.axis_index("dp")
    me = lax.axis_index("context")
    head = lax.axis_index("head")
    other = 1 - head
    rows2, features = tok_ref.shape
    rows = rows2 // 2
    wrows = wk_ref.shape[0]
    half = n // 2
    score_scale = 1.0 / math.sqrt(HEAD_DIM)
    drains = []

    def copy_of(src, dst, send_sem, recv_sem, **device):
        return pltpu.make_async_remote_copy(
            src_ref=src, dst_ref=dst, send_sem=send_sem, recv_sem=recv_sem,
            device_id=device, device_id_type=MESH,
        )

    def put(src, dst, send_sem, recv_sem, **device):
        copy_of(src, dst, send_sem, recv_sem, **device).start()

    def put_if(condition, src, dst, send_sem, recv_sem, **device):
        pl.when(condition)(copy_of(src, dst, send_sem, recv_sem, **device).start)

    def arrived(dst, recv_sem):
        copy_of(dst, dst, loc_sem.at[0], recv_sem, head=other).wait_recv()

    def drain(whole, send_sem, condition=None):
        drains.append((condition, copy_of(whole, whole, send_sem, loc_sem.at[0], head=other)))

    def slot(src, dst):
        return lax.rem(src - dst + n - 1, n)

    def inside(place):
        return (place >= 0) & (place < n)

    def dp_slot(src, dst):
        return lax.rem(src - dst + m - 1, m)

    near = line_order(me, n)
    far = near[::-1]
    sides = (me + 1, me - 1)
    dp_peers = [lax.rem(me_dp + off, m) for off in range(1, m)]

    two_step = m == 4 and share % 32 == 0
    if two_step:
        low = lax.rem(me_dp, 2)
        w_peers = [(0, me_dp + 1 - 2 * low), (1, lax.rem(me_dp + 2, 4))]
    else:
        w_peers = list(enumerate(dp_peers))

    w_copies = [
        pltpu.make_async_copy(wk_ref, wf.at[me, :, pl.ds(0, HEAD_DIM)], loc_sem.at[0]),
        pltpu.make_async_copy(wv_ref, wf.at[me, :, pl.ds(HEAD_DIM, HEAD_DIM)], loc_sem.at[0]),
    ]
    own_half = pltpu.make_async_copy(tok_ref, tokf.at[head], loc_sem.at[1])
    row_copies = [
        pltpu.make_async_copy(q_in, qg.at[0], loc_sem.at[2]),
        pltpu.make_async_copy(g_in, qg.at[1], loc_sem.at[2]),
    ]
    for copy in w_copies + [own_half] + row_copies:
        copy.start()
    barrier = pltpu.get_barrier_semaphore()
    for _, peer in near:
        pl.semaphore_signal(barrier, inc=1, device_id={"context": peer}, device_id_type=MESH)
    for peer in dp_peers:
        pl.semaphore_signal(barrier, inc=1, device_id={"dp": peer}, device_id_type=MESH)
    pl.semaphore_signal(barrier, inc=1, device_id={"head": other}, device_id_type=MESH)
    pl.semaphore_wait(barrier, n + m - 1)

    def cores_meet():
        pl.semaphore_signal(pair_sem, inc=1, device_id={"head": other}, device_id_type=MESH)
        pl.semaphore_wait(pair_sem, 1)

    shared_base = pl.multiple_of(me_dp * share, 16)
    chunks = 2 if two_step else 1
    piece_rows = share // chunks

    def w_piece(owner, base, chunk):
        return wf.at[owner, pl.ds(pl.multiple_of(base + chunk * piece_rows, 16), piece_rows)]

    direct_rows = wrows - m * share
    direct = pl.ds(m * share, direct_rows)
    pltpu.make_async_copy(wf.at[me], wf.at[me], loc_sem.at[0]).wait()
    share_rows = wf.at[0, pl.ds(0, share)]
    for chunk in range(chunks):
        part = w_piece(me, shared_base, chunk)
        for at, peer in enumerate(sides):
            put_if(inside(peer), part, part, wz_s.at[at], wz_r.at[slot(me, peer), chunk], context=peer)
    for at, peer in enumerate(sides):
        drain(share_rows, wz_s.at[at], inside(peer))
    own_half.wait()
    put(tokf.at[head], tokf.at[head], tok_sem.at[0], tok_sem.at[1], head=other)
    drain(tokf.at[head], tok_sem.at[0])
    if direct_rows:
        for k, peer in near:
            part = wf.at[me, direct]
            put(part, part, wd_s.at[k - 1], wd_r.at[slot(me, peer)], context=peer)
            drain(part, wd_s.at[k - 1])

    def token_block(owner):
        column = pl.multiple_of(lax.rem(owner, half) * wrows, 128)
        return owner // half, pl.ds(column, wrows)

    quarter = rows // 4
    base = me // half * half
    place = me - base
    mates = [base + lax.rem(place + k, half) for k in range(1, half)]
    cross = [jnp.where(me < half, half + k, half - 1 - k) for k in range(half)]
    partner = lax.rem(me + half, n)
    outer = (me == 0) | (me == n - 1)
    inner = (me > 0) & (me < n - 1)

    def mate_slot(src, dst):
        return lax.rem(src - dst + half - 1, half)

    def cross_rows(core, part):
        return pl.ds(pl.multiple_of(core * 2 * quarter + part * quarter, 16), quarter)

    def mate_rows(core, part):
        if part == 0:
            return pl.ds(pl.multiple_of(core * rows, 16), rows)
        return pl.ds(pl.multiple_of(core * 2 * quarter, 16), 2 * quarter)

    def cross_copy(part, peer):
        span = cross_rows(head, part)
        side, columns = token_block(peer)
        return copy_of(
            tokf.at[side, span, columns], tokd.at[me, span],
            t1_s.at[part], t1_r.at[part, lax.rem(me, half)], context=peer,
        )

    def mate_copy(part, peer):
        if part == 0:
            side, columns = token_block(peer)
            span = mate_rows(head, 0)
            held = tokd.at[me, span]
        else:
            side, columns = token_block(lax.rem(peer + half, n))
            span = pl.ds(pl.multiple_of(rows + head * 2 * quarter, 16), 2 * quarter)
            held = tokn.at[place, mate_rows(head, 1)]
        return copy_of(
            tokf.at[side, span, columns], held,
            t2_s.at[part], t2_r.at[part, mate_slot(me, peer)], context=peer,
        )

    my_side, my_columns = token_block(me)

    def w_forward(src):
        for dp_at, peer in w_peers:
            part = w_piece(src, peer * share, dp_at)
            arrived(part, wx_r.at[slot(src, me), 2 * dp_at + dp_at])
            to = w_peers[1 - dp_at][1]
            put(part, part, wx_s.at[slot(src, me)], wx_r.at[slot(src, me), 4 + dp_at], dp=to)

    for k, src in near:
        onward = jnp.where(src > me, me - 1, me + 1)
        for chunk in range(chunks):
            part = w_piece(src, shared_base, chunk)
            arrived(part, wz_r.at[slot(src, me), chunk])
            put_if(inside(onward), part, part, wz_s.at[1 + k], wz_r.at[slot(src, onward), chunk], context=onward)
            for dp_at, peer in w_peers:
                put(part, part, wx_s.at[slot(src, me)], wx_r.at[slot(src, me), chunks * dp_at + chunk], dp=peer)
        drain(share_rows, wz_s.at[1 + k], inside(onward))
        drain(wf.at[0, pl.ds(0, (m - 1) * share)], wx_s.at[slot(src, me)])
        if k == 1:
            arrived(tokf.at[other], tok_sem.at[1])
            for peer in mates:
                for part in range(2):
                    pl.when(outer)(mate_copy(part, peer).start)
        if two_step and k > 1:
            w_forward(near[k - 2][1])
    cores_meet()
    for peer in cross[::-1]:
        cross_copy(0, peer).start()
    for peer in cross[::-1]:
        pl.when(peer < me)(cross_copy(1, peer).start)
    for peer in mates:
        pl.when(inner)(mate_copy(1, peer).start)
        pl.when((peer < me) & inner)(mate_copy(0, peer).start)
    own_tokens = pltpu.make_async_copy(tokf.at[my_side, :, my_columns], tokd.at[me], loc_sem.at[3])
    own_tokens.start()
    for part in range(2):
        held = tokd.at[pl.ds(0, half), pl.ds(0, quarter)]
        drain(held, t1_s.at[part])
        drain(held, f1_s.at[part])
    for part, held in enumerate((tokd.at[pl.ds(0, half - 1), pl.ds(0, rows)], tokn.at[pl.ds(0, half - 1), pl.ds(0, 2 * quarter)])):
        drain(held, t2_s.at[part])
        drain(held, f2_s.at[part])
    if two_step:
        w_forward(near[-1][1])

    projected = dot(tokf[my_side, :, my_columns], wf[me])
    for k, src in near:
        if direct_rows:
            arrived(wf.at[src, direct], wd_r.at[slot(src, me)])
        if two_step:
            for dp_at, peer in w_peers:
                part = w_piece(src, peer * share, 1 - dp_at)
                arrived(part, wx_r.at[slot(src, me), 2 * dp_at + 1 - dp_at])
                part = w_piece(src, (3 - me_dp) * share, dp_at)
                arrived(part, wx_r.at[slot(src, me), 4 + dp_at])
        else:
            for off in range(1, m):
                part = w_piece(src, lax.rem(me_dp + m - off, m) * share, 0)
                arrived(part, wx_r.at[slot(src, me), off - 1])
        side, columns = token_block(src)
        projected += dot(tokf[side, :, columns], wf[src])
    pairs = projected.astype(jnp.bfloat16)
    my_rows = pl.ds(pl.multiple_of(me * rows, rows), rows)
    kv[my_rows, :] = pairs[:rows]
    kvn[...] = pairs[rows:]
    for k, peer in far:
        put_if(peer > me, kv.at[my_rows], kv.at[my_rows], kv_s.at[k - 1], kv_r.at[slot(me, peer)], context=peer)
        drain(kv.at[my_rows], kv_s.at[k - 1], peer > me)
    put(wf.at[pl.ds(other * half, half)], wo, wo_sem.at[0], wo_sem.at[1], head=other)
    drain(wo, wo_sem.at[0])

    block = blk_ref[0]
    total_rows = n * rows
    lane = lax.broadcasted_iota(jnp.int32, (1, rows2), 1)
    noisy_lane = lane >= rows
    position = me * rows + jnp.where(noisy_lane, lane - rows, lane)
    block_start = position & (-block)
    limit = jnp.where(noisy_lane, block_start, block_start + block)
    dkv[...] = jnp.zeros_like(dkv)
    dn[...] = jnp.zeros_like(dn)
    knt[...] = kvn[:, :HEAD_DIM].T
    pltpu.make_async_copy(qg, qg, loc_sem.at[2]).wait()
    for k, src in near:
        span = pl.ds(pl.multiple_of(src * rows, rows), rows)

        @pl.when(src < me)
        def _(span=span, src=src):
            arrived(kv.at[span], kv_r.at[slot(src, me)])

        @pl.when(src > me)
        def _(span=span):
            kv[span, :] = jnp.zeros((rows, 2 * HEAD_DIM), jnp.bfloat16)
    for _, peer in near:

        @pl.when(peer < me)
        def _(peer=peer):
            pl.semaphore_signal(kv_credit, inc=1, device_id={"context": peer}, device_id_type=MESH)

    kt[...] = kv[:, :HEAD_DIM].T

    steps = 4 if n % 4 == 0 else 1
    step_rows = total_rows // steps

    def head_turns(first, last):
        for step in range(steps):

            @pl.when(me // (n // steps) == step)
            def _(step=step):
                turn_of = functools.partial(head_turn, (step + 1) * step_rows)
                lax.fori_loop(first, last, turn_of, 0)

    def head_turn(extent, turn, carry):
        open_rows = extent - step_rows
        columns = pl.ds(pl.multiple_of(turn * HEAD_DIM, HEAD_DIM), HEAD_DIM)
        q = qg[0, :, columns]
        g = qg[1, :, columns]
        keys = kv[:extent, :HEAD_DIM]
        values = kv[:extent, HEAD_DIM:]
        own_keys = kvn[:, :HEAD_DIM]
        own_values = kvn[:, HEAD_DIM:]
        key_pos = open_rows + lax.broadcasted_iota(jnp.int32, (step_rows, rows2), 0)
        near = lax.broadcasted_iota(jnp.int32, (rows, rows), 0)
        same = (near ^ lax.broadcasted_iota(jnp.int32, (rows, rows), 1)) < block
        s = dot_nt(keys, q) * score_scale
        s_edge = jnp.where(key_pos < limit, s[open_rows:], MASKED)
        s = jnp.concatenate([s[:open_rows], s_edge], axis=0) if open_rows else s_edge
        s_own = jnp.where(same, dot_nt(own_keys, q[rows:]) * score_scale, MASKED)
        peak = jnp.max(s, axis=0, keepdims=True)
        peak_own = jnp.maximum(peak[:, rows:], jnp.max(s_own, axis=0, keepdims=True))
        peak = jnp.concatenate([peak[:, :rows], peak_own], axis=1)
        e = jnp.exp(s - peak)
        e_own = jnp.exp(s_own - peak_own)
        total = jnp.sum(e, axis=0, keepdims=True)
        total_own = total[:, rows:] + jnp.sum(e_own, axis=0, keepdims=True)
        inverse = 1.0 / jnp.concatenate([total[:, :rows], total_own], axis=1)
        p = e * inverse
        p_own = e_own * inverse[:, rows:]
        p_half = p.astype(jnp.bfloat16)
        p_half_own = p_own.astype(jnp.bfloat16)
        gp = dot_nt(values, g)
        gp_own = dot_nt(own_values, g[rows:])
        delta = jnp.sum(p_half.astype(jnp.float32) * gp, axis=0, keepdims=True)
        delta_own = delta[:, rows:] + jnp.sum(
            p_half_own.astype(jnp.float32) * gp_own, axis=0, keepdims=True
        )
        delta = jnp.concatenate([delta[:, :rows], delta_own], axis=1)
        ds = (p * (gp - delta)).astype(jnp.bfloat16)
        ds_own = (p_own * (gp_own - delta_own)).astype(jnp.bfloat16)
        dkv[:extent, :HEAD_DIM] += dot(ds, q)
        dkv[:extent, HEAD_DIM:] += dot(p_half, g)
        dn[:, :HEAD_DIM] += dot(ds_own, q[rows:])
        dn[:, HEAD_DIM:] += dot(p_half_own, g[rows:])
        dq = dot(kt[:, :extent], ds)
        dq_own = dq[:, rows:] + dot(knt[...], ds_own)
        dq_ref[:rows, columns] = (dq[:, :rows] * score_scale).T.astype(jnp.bfloat16)
        dq_ref[rows:, columns] = (dq_own * score_scale).T.astype(jnp.bfloat16)
        return carry

    turns = qg.shape[2] // HEAD_DIM
    head_turns(0, turns * 5 // 8)

    @pl.when(me < n - 1)
    def _():
        pl.semaphore_wait(kv_credit, n - 1 - me)

    for peer in cross[::-1]:
        pl.when(peer > me)(cross_copy(1, peer).start)
    head_turns(turns * 5 // 8, turns)

    pair_scale = jnp.where(
        lax.broadcasted_iota(jnp.int32, (1, 2 * HEAD_DIM), 1) < HEAD_DIM, score_scale, 1.0
    )
    clean, noisy = pl.ds(0, rows), pl.ds(rows, rows)
    pga[me, noisy] = (dn[...] * pair_scale).astype(jnp.bfloat16)
    for peer in mates:
        part = pga.at[me, noisy]
        put(part, part, pg_s.at[0], pn_r.at[mate_slot(me, peer)], context=peer)
    for block_at in range(n):
        pgp[block_at] = (dkv[block_at * rows : (block_at + 1) * rows] * pair_scale).astype(jnp.bfloat16)
    for k, peer in far:
        put_if(peer < me, pgp.at[peer], pin.at[me], pp_s.at[k - 1], pp_r.at[slot(me, peer)], context=peer)
        drain(pgp.at[peer], pp_s.at[k - 1], peer < me)


    def clean_copy(peer):
        part = pga.at[me, clean]
        return copy_of(part, part, pg_s.at[1], pc_r.at[slot(me, peer)], context=peer)

    for peer in mates:
        pl.when((peer > me) & inner)(mate_copy(0, peer).start)
    put(pga.at[me, noisy], pgo.at[noisy], po_sem.at[0], po_sem.at[1], head=other)
    dkv[my_rows, :] *= pair_scale

    def cross_onward(src, part):
        held = tokd.at[src, cross_rows(head, part)]
        arrived(held, t1_r.at[part, lax.rem(src, half)])
        put(held, held, f1_s.at[part], f1_r.at[part, lax.rem(src, half)], head=other)

    def mate_held(src, core, part):
        return tokd.at[src, mate_rows(core, 0)] if part == 0 else tokn.at[src - base, mate_rows(core, 1)]

    def mate_onward(src, part):
        held = mate_held(src, head, part)
        arrived(held, t2_r.at[part, mate_slot(src, me)])
        put(held, held, f2_s.at[part], f2_r.at[part, mate_slot(src, me)], head=other)

    for src in mates:
        mate_onward(src, 1)
    for src in cross:
        cross_onward(src, 0)
    foreign_side, foreign_columns = token_block(partner)
    gf = dot(pga[me, noisy].T, tokf[foreign_side, rows:, foreign_columns])
    for src in mates:
        arrived(mate_held(src, other, 1), f2_r.at[1, mate_slot(src, me)])
        arrived(pga.at[src, noisy], pn_r.at[mate_slot(src, me)])
        gf += dot(pga[src, noisy].T, tokn[src - base])
    slab = gf.shape[0] // m
    for at in range(m):
        gsum[at] = gf[at * slab : (at + 1) * slab]
        fp[at] = gf[at * slab : (at + 1) * slab].astype(jnp.bfloat16)
    foreign_own[...] = gsum[me_dp]
    for peer in dp_peers:
        put(fp.at[peer], fin.at[me_dp], rf_s.at[0], rf_r.at[dp_slot(me_dp, peer)], dp=peer)
    drain(fp.at[pl.ds(0, m - 1)], rf_s.at[0])
    for k, src in near:

        @pl.when(src > me)
        def _(src=src):
            arrived(pin.at[src], pp_r.at[slot(src, me)])
            dkv[my_rows, :] += pin[src].astype(jnp.float32)

    for _, peer in near:

        @pl.when((me == 0) & (peer > 1))
        def _(peer=peer):
            pl.semaphore_signal(pin_credit, inc=1, device_id={"context": peer}, device_id_type=MESH)

    pga[me, clean] = dkv[my_rows, :].astype(jnp.bfloat16)
    for k, peer in far:
        pl.when(peer > me)(clean_copy(peer).start)
    for k, peer in near:
        pl.when((peer < me) & (peer > 0))(clean_copy(peer).start)

    @pl.when(me > 1)
    def _():
        pl.semaphore_wait(pin_credit, 1)

    for k, peer in near:
        pl.when((peer < me) & (peer == 0))(clean_copy(peer).start)
    put(pga.at[me, clean], pgo.at[clean], po_sem.at[0], po_sem.at[2], head=other)
    drain(pga.at[pl.ds(0, half - 1), noisy], pg_s.at[0])
    drain(pga.at[pl.ds(0, n - 1), clean], pg_s.at[1])
    drain(pga.at[me], po_sem.at[0])

    own_tokens.wait()
    for src in mates:
        mate_onward(src, 0)
    for src in cross:
        cross_onward(src, 1)
    gw = dot(pga[me].T, tokd[me])
    for src in mates:
        arrived(mate_held(src, other, 0), f2_r.at[0, mate_slot(src, me)])
        arrived(pga.at[src, clean], pc_r.at[slot(src, me)])
        gw += dot(pga[src].T, tokd[src])
    for src in cross:
        for part in range(2):
            arrived(tokd.at[src, cross_rows(other, part)], f1_r.at[part, lax.rem(src, half)])
        arrived(pga.at[src, clean], pc_r.at[slot(src, me)])
        gw += dot(pga[src, clean].T, tokd[src, clean])

    for at in range(m):
        gsum[at] = gw[at * slab : (at + 1) * slab]
        rp[at] = gw[at * slab : (at + 1) * slab].astype(jnp.bfloat16)
    for peer in dp_peers:
        put(rp.at[peer], rin.at[me_dp], rs_s.at[0], rs_r.at[dp_slot(me_dp, peer)], dp=peer)
    drain(rp.at[pl.ds(0, m - 1)], rs_s.at[0])
    foreign_sum = foreign_own[...]
    for src in dp_peers:
        arrived(fin.at[src], rf_r.at[dp_slot(src, me_dp)])
        foreign_sum += fin[src].astype(jnp.float32)
    zout[...] = foreign_sum.astype(jnp.bfloat16)
    put(zout, zin, z_sem.at[0], z_sem.at[1], context=partner)
    drain(zout, z_sem.at[0])
    arrived(wo, wo_sem.at[1])
    arrived(pgo.at[noisy], po_sem.at[1])
    arrived(pgo.at[clean], po_sem.at[2])
    for at in range(half):
        gx_ref[:, at * wrows : (at + 1) * wrows] = (
            dot_nt(pga[me], wf[head * half + at]) + dot_nt(pgo[...], wo[at])
        ).astype(jnp.bfloat16)

    slab_sum = gsum[me_dp]
    for src in dp_peers:
        arrived(rin.at[src], rs_r.at[dp_slot(src, me_dp)])
        slab_sum += rin[src].astype(jnp.float32)
    arrived(zin, z_sem.at[1])
    slab_sum += zin[...].astype(jnp.float32)
    rall[me_dp] = slab_sum.astype(jnp.bfloat16)
    for peer in dp_peers:
        put(rall.at[me_dp], rall.at[me_dp], ra_s.at[0], ra_r.at[dp_slot(me_dp, peer)], dp=peer)
    drain(rall.at[pl.ds(0, m - 1)], ra_s.at[0])
    for src in dp_peers:
        arrived(rall.at[src], ra_r.at[dp_slot(src, me_dp)])
    for at in range(m):
        gsum[at] = rall[at].astype(jnp.float32)
    gwk_ref[...] = gsum[: m // 2].reshape(HEAD_DIM, wrows).T
    gwv_ref[...] = gsum[m // 2 :].reshape(HEAD_DIM, wrows).T
    for condition, copy in drains:
        if condition is None:
            copy.wait_send()
        else:
            pl.when(condition)(copy.wait_send)


def store_kernel(dq_in, gx_in, gwk_in, gwv_in, dq_out, gx_out, gwk_out, gwv_out, sem):
    pairs = ((gx_in, gx_out), (dq_in, dq_out), (gwk_in, gwk_out), (gwv_in, gwv_out))
    copies = [pltpu.make_async_copy(src, dst, sem.at[at]) for at, (src, dst) in enumerate(pairs)]
    for copy in copies:
        copy.start()
    for copy in copies:
        copy.wait()


def per_device(tokens, queries, grad_out, w_key, w_value, block_len):
    n = lax.axis_size("context")
    m = lax.axis_size("dp")
    rows = tokens.shape[2]
    features = tokens.shape[3]
    wrows, width = w_key.shape
    q_width = queries.shape[3]
    share = wrows // m // 16 * 16
    direct_slots = n - 1 if wrows > m * share else 1
    half = n // 2
    pair = 2 * width
    bf16, f32 = jnp.bfloat16, jnp.float32
    vmem = pl.BlockSpec(memory_space=pltpu.VMEM)
    dma = pltpu.SemaphoreType.DMA
    hbm = pl.BlockSpec(memory_space=pltpu.HBM)
    slab = pair // m
    results = (
        ((2 * rows, q_width), bf16),
        ((2 * rows, features), bf16),
        ((wrows, width), f32),
        ((wrows, width), f32),
    )
    dq, gx, gwk, gwv = pl.pallas_call(
        functools.partial(fused_kernel, n, m, share),
        out_shape=tuple(pltpu.VMEM(*result) for result in results),
        in_specs=[pl.BlockSpec(memory_space=pltpu.SMEM)] + [hbm] * 5,
        out_specs=(vmem, vmem, vmem, vmem),
        scratch_shapes=[
            pltpu.VMEM((2, 2 * rows, q_width), bf16),
            pltpu.VMEM((2, 2 * rows, features), bf16),
            pltpu.VMEM((n, wrows, pair), bf16),
            pltpu.VMEM((half, wrows, pair), bf16),
            pltpu.VMEM((n * rows, pair), bf16),
            pltpu.VMEM((rows, pair), bf16),
            pltpu.VMEM((width, n * rows), bf16),
            pltpu.VMEM((width, rows), bf16),
            pltpu.VMEM((n * rows, pair), f32),
            pltpu.VMEM((rows, pair), f32),
            pltpu.VMEM((n, rows, pair), bf16),
            pltpu.VMEM((n, rows, pair), bf16),
            pltpu.VMEM((n, 2 * rows, pair), bf16),
            pltpu.VMEM((2 * rows, pair), bf16),
            pltpu.VMEM((n, 2 * rows, wrows), bf16),
            pltpu.VMEM((half, rows, wrows), bf16),
            pltpu.VMEM((m, slab, wrows), f32),
            pltpu.VMEM((m, slab, wrows), bf16),
            pltpu.VMEM((m, slab, wrows), bf16),
            pltpu.VMEM((m, slab, wrows), bf16),
            pltpu.VMEM((m, slab, wrows), bf16),
            pltpu.VMEM((m, slab, wrows), bf16),
            pltpu.VMEM((slab, wrows), f32),
            pltpu.VMEM((slab, wrows), bf16),
            pltpu.VMEM((slab, wrows), bf16),
            dma((4,)), pltpu.SemaphoreType.REGULAR, pltpu.SemaphoreType.REGULAR, pltpu.SemaphoreType.REGULAR, dma((2,)),
            dma((n + 1,)), dma((n - 1, 2)), dma((direct_slots,)), dma((direct_slots,)),
            dma((n - 1,)), dma((n - 1, max(6, m - 1))), dma((2,)), dma((n - 1,)), dma((n - 1,)),
            dma((2,)), dma((2, half)), dma((2,)), dma((2, half)),
            dma((2,)), dma((2, half - 1)), dma((2,)), dma((2, half - 1)), dma((n - 1,)), dma((n - 1,)),
            dma((2,)), dma((half - 1,)), dma((n - 1,)), dma((3,)),
            dma((1,)), dma((m - 1,)), dma((2,)), dma((1,)), dma((m - 1,)), dma((1,)), dma((m - 1,)),
        ],
        compiler_params=pltpu.CompilerParams(
            collective_id=0, has_side_effects=True, vmem_limit_bytes=VMEM_LIMIT
        ),
    )(
        block_len,
        tokens.reshape(2 * rows, features),
        queries.reshape(2 * rows, q_width),
        grad_out.reshape(2 * rows, q_width),
        w_key,
        w_value,
    )
    dq, gx, gwk, gwv = pl.pallas_call(
        store_kernel,
        out_shape=tuple(jax.ShapeDtypeStruct(*result) for result in results),
        in_specs=[vmem] * 4,
        out_specs=(hbm, hbm, hbm, hbm),
        scratch_shapes=[dma((4,))],
    )(*(pltpu.with_memory_space_constraint(x, pltpu.VMEM) for x in (dq, gx, gwk, gwv)))
    return (
        dq.reshape(queries.shape),
        gx.reshape(tokens.shape),
        gwk,
        gwv,
    )


def solution(mesh):
    placed = (
        P("dp", None, "context", "head"),
        P("dp", None, "context", "head"),
        P("dp", None, "context", "head"),
        P("context", "head"),
        P("context", "head"),
        P("dp"),
    )
    return jax.shard_map(
        per_device,
        mesh=mesh,
        in_specs=placed,
        out_specs=(
            P("dp", None, "context", "head"),
            P("dp", None, "context", "head"),
            P("context", "head"),
            P("context", "head"),
        ),
        check_vma=False,
    )
```

time: 76.4 us -> 71.3 us (0.933)
  Pallas kernels: 75 us -> 69.9 us
    pallas_call x1, Pallas kernels: 73.5 us -> 68.3 us  [per_device(): pl.pallas_call(functools.partial(fused_kernel, n, m, share), out_shape=tu...]
where the time goes in v2:
time: 71.3 us; the launch traced here: 71.1 us
  Pallas kernels  69.9 us (98%)
  between operations  1.29 us (2%)
    pallas_call x1, Pallas kernels, per_device(): pl.pallas_call(functools.partial(fused_kernel, n, m, share), out_shape=tu...  68.3 us
    pallas_call x1, Pallas kernels, per_device(): pl.pallas_call(store_kernel, out_shape=tuple((jax.ShapeDtypeStruct(*resul...  1.52 us

profile of v2, /device:TPU:0, one launch (start us, length us, event | category | flops | bytes accessed | tf_op | source)
XLA Modules:
  0.0 71.1 jit_solution(10049239496161308139)
XLA Ops:
  1.3 68.3 %shard_map.93 = (bf16[256,1024]{1,0:T(8,128)(2,1)S(1)}, bf16[256,2048]{1,0:T(8,128)(2,1)S(1)}, f32[1024,128]{1,0:T(8,128)S(1)}, f32[1024,128]{1,0:T(8,128)S(1)}) custom-call(s32[1]{0:T(128)S(6)} %copy.10.blk_ref, bf16[256,2048]{1,0:T(8,128)(2,1)} %bitcast.5, bf16[256,1024]{1,0:T(8,128)(2,1)} %bitcast.6, bf16[256,1024]{1,0:T(8,128)(2,1)} %bitcast.7, ...), custom_call_target="tpu_custom_call" | custom-call | tf_op jit(solution)/shard_map/pallas_call | solution.py:539
  69.6 1.5 %shard_map.94 = (bf16[256,1024]{1,0:T(8,128)(2,1)}, bf16[256,2048]{1,0:T(8,128)(2,1)}, f32[1024,128]{1,0:T(8,128)}, f32[1024,128]{1,0:T(8,128)}) custom-call(bf16[256,1024]{1,0:T(8,128)(2,1)S(1)} %get-tuple-element.12.dq_in, bf16[256,2048]{1,0:T(8,128)(2,1)S(1)} %get-tuple-element.13.gx_in, f32[1024,128]{1,0:T(8,128)S(1)} %get-tuple-element.14.gwk_in, ...), custom_call_target="tpu_custom_call" | custom-call | tf_op jit(solution)/shard_map/pallas_call | solution.py:589

commit v3 on v2

--- a/solution.py
+++ b/solution.py
@@ -36,12 +36,12 @@
 
 
 def fused_kernel(
-    n, m, share,
+    n, m, share, pack,
     blk_ref, tok_ref, q_in, g_in, wk_ref, wv_ref,
     dq_ref, gx_ref, gwk_ref, gwv_ref,
     qg, tokf, wf, wo, kv, kvn, kt, knt, dkv, dn, pgp, pin, pga, pgo, tokd, tokn,
     gsum, rp, rin, rall, fp, fin, foreign_own, zout, zin,
-    loc_sem, pair_sem, kv_credit, pin_credit, tok_sem, wz_s, wz_r, wd_s, wd_r, wx_s, wx_r, wo_sem, kv_s, kv_r,
+    loc_sem, pair_sem, kv_credit, tok_sem, wz_s, wz_r, wd_s, wd_r, wx_s, wx_r, wo_sem, kv_s, kv_r,
     t1_s, t1_r, f1_s, f1_r, t2_s, t2_r, f2_s, f2_r, pp_s, pp_r, pg_s, pn_r, pc_r, po_sem,
     rf_s, rf_r, z_sem, rs_s, rs_r, ra_s, ra_r,
 ):
@@ -264,9 +264,9 @@
 
     block = blk_ref[0]
     total_rows = n * rows
-    lane = lax.broadcasted_iota(jnp.int32, (1, rows2), 1)
-    noisy_lane = lane >= rows
-    position = me * rows + jnp.where(noisy_lane, lane - rows, lane)
+    lane = lax.broadcasted_iota(jnp.int32, (1, pack * rows2), 1)
+    noisy_lane = lane >= pack * rows
+    position = me * rows + lane % rows
     block_start = position & (-block)
     limit = jnp.where(noisy_lane, block_start, block_start + block)
     dkv[...] = jnp.zeros_like(dkv)
@@ -302,55 +302,65 @@
                 turn_of = functools.partial(head_turn, (step + 1) * step_rows)
                 lax.fori_loop(first, last, turn_of, 0)
 
+    wide = pack * rows
+
     def head_turn(extent, turn, carry):
         open_rows = extent - step_rows
-        columns = pl.ds(pl.multiple_of(turn * HEAD_DIM, HEAD_DIM), HEAD_DIM)
-        q = qg[0, :, columns]
-        g = qg[1, :, columns]
+        spans = [
+            pl.ds(pl.multiple_of((turn * pack + at) * HEAD_DIM, HEAD_DIM), HEAD_DIM) for at in range(pack)
+        ]
+
+        def stacked(which):
+            held = [qg[which, :, span] for span in spans]
+            return jnp.concatenate([x[:rows] for x in held] + [x[rows:] for x in held], axis=0)
+
+        q = stacked(0)
+        g = stacked(1)
         keys = kv[:extent, :HEAD_DIM]
         values = kv[:extent, HEAD_DIM:]
         own_keys = kvn[:, :HEAD_DIM]
         own_values = kvn[:, HEAD_DIM:]
-        key_pos = open_rows + lax.broadcasted_iota(jnp.int32, (step_rows, rows2), 0)
-        near = lax.broadcasted_iota(jnp.int32, (rows, rows), 0)
-        same = (near ^ lax.broadcasted_iota(jnp.int32, (rows, rows), 1)) < block
-        s = dot_nt(keys, q) * score_scale
+        key_pos = open_rows + lax.broadcasted_iota(jnp.int32, (step_rows, 2 * wide), 0)
+        near_key = lax.broadcasted_iota(jnp.int32, (rows, wide), 0)
+        near_row = lax.broadcasted_iota(jnp.int32, (rows, wide), 1) % rows
+        same = (near_key ^ near_row) < block
+        s = dot_nt(keys, q)
         s_edge = jnp.where(key_pos < limit, s[open_rows:], MASKED)
         s = jnp.concatenate([s[:open_rows], s_edge], axis=0) if open_rows else s_edge
-        s_own = jnp.where(same, dot_nt(own_keys, q[rows:]) * score_scale, MASKED)
+        s_own = jnp.where(same, dot_nt(own_keys, q[wide:]), MASKED)
         peak = jnp.max(s, axis=0, keepdims=True)
-        peak_own = jnp.maximum(peak[:, rows:], jnp.max(s_own, axis=0, keepdims=True))
-        peak = jnp.concatenate([peak[:, :rows], peak_own], axis=1)
-        e = jnp.exp(s - peak)
-        e_own = jnp.exp(s_own - peak_own)
+        peak_own = jnp.maximum(peak[:, wide:], jnp.max(s_own, axis=0, keepdims=True))
+        peak = jnp.concatenate([peak[:, :wide], peak_own], axis=1)
+        e = jnp.exp((s - peak) * score_scale)
+        e_own = jnp.exp((s_own - peak_own) * score_scale)
         total = jnp.sum(e, axis=0, keepdims=True)
-        total_own = total[:, rows:] + jnp.sum(e_own, axis=0, keepdims=True)
-        inverse = 1.0 / jnp.concatenate([total[:, :rows], total_own], axis=1)
+        total_own = total[:, wide:] + jnp.sum(e_own, axis=0, keepdims=True)
+        inverse = 1.0 / jnp.concatenate([total[:, :wide], total_own], axis=1)
         p = e * inverse
-        p_own = e_own * inverse[:, rows:]
+        p_own = e_own * inverse[:, wide:]
         p_half = p.astype(jnp.bfloat16)
         p_half_own = p_own.astype(jnp.bfloat16)
-        gp = dot_nt(values, g)
-        gp_own = dot_nt(own_values, g[rows:])
-        delta = jnp.sum(p_half.astype(jnp.float32) * gp, axis=0, keepdims=True)
-        delta_own = delta[:, rows:] + jnp.sum(
-            p_half_own.astype(jnp.float32) * gp_own, axis=0, keepdims=True
-        )
-        delta = jnp.concatenate([delta[:, :rows], delta_own], axis=1)
-        ds = (p * (gp - delta)).astype(jnp.bfloat16)
-        ds_own = (p_own * (gp_own - delta_own)).astype(jnp.bfloat16)
+        weighted = p * dot_nt(values, g)
+        weighted_own = p_own * dot_nt(own_values, g[wide:])
+        delta = jnp.sum(weighted, axis=0, keepdims=True)
+        delta_own = delta[:, wide:] + jnp.sum(weighted_own, axis=0, keepdims=True)
+        delta = jnp.concatenate([delta[:, :wide], delta_own], axis=1)
+        ds = (weighted - p * delta).astype(jnp.bfloat16)
+        ds_own = (weighted_own - p_own * delta_own).astype(jnp.bfloat16)
         dkv[:extent, :HEAD_DIM] += dot(ds, q)
         dkv[:extent, HEAD_DIM:] += dot(p_half, g)
-        dn[:, :HEAD_DIM] += dot(ds_own, q[rows:])
-        dn[:, HEAD_DIM:] += dot(p_half_own, g[rows:])
+        dn[:, :HEAD_DIM] += dot(ds_own, q[wide:])
+        dn[:, HEAD_DIM:] += dot(p_half_own, g[wide:])
         dq = dot(kt[:, :extent], ds)
-        dq_own = dq[:, rows:] + dot(knt[...], ds_own)
-        dq_ref[:rows, columns] = (dq[:, :rows] * score_scale).T.astype(jnp.bfloat16)
-        dq_ref[rows:, columns] = (dq_own * score_scale).T.astype(jnp.bfloat16)
+        dq_own = dq[:, wide:] + dot(knt[...], ds_own)
+        for at, span in enumerate(spans):
+            lanes = slice(at * rows, (at + 1) * rows)
+            dq_ref[:rows, span] = (dq[:, lanes] * score_scale).T.astype(jnp.bfloat16)
+            dq_ref[rows:, span] = (dq_own[:, lanes] * score_scale).T.astype(jnp.bfloat16)
         return carry
 
-    turns = qg.shape[2] // HEAD_DIM
-    head_turns(0, turns * 5 // 8)
+    turns = qg.shape[2] // HEAD_DIM // pack
+    head_turns(0, turns // 2)
 
     @pl.when(me < n - 1)
     def _():
@@ -358,7 +368,7 @@
 
     for peer in cross[::-1]:
         pl.when(peer > me)(cross_copy(1, peer).start)
-    head_turns(turns * 5 // 8, turns)
+    head_turns(turns // 2, turns)
 
     pair_scale = jnp.where(
         lax.broadcasted_iota(jnp.int32, (1, 2 * HEAD_DIM), 1) < HEAD_DIM, score_scale, 1.0
@@ -422,24 +432,13 @@
             arrived(pin.at[src], pp_r.at[slot(src, me)])
             dkv[my_rows, :] += pin[src].astype(jnp.float32)
 
-    for _, peer in near:
-
-        @pl.when((me == 0) & (peer > 1))
-        def _(peer=peer):
-            pl.semaphore_signal(pin_credit, inc=1, device_id={"context": peer}, device_id_type=MESH)
-
     pga[me, clean] = dkv[my_rows, :].astype(jnp.bfloat16)
     for k, peer in far:
         pl.when(peer > me)(clean_copy(peer).start)
-    for k, peer in near:
-        pl.when((peer < me) & (peer > 0))(clean_copy(peer).start)
-
-    @pl.when(me > 1)
-    def _():
-        pl.semaphore_wait(pin_credit, 1)
-
-    for k, peer in near:
-        pl.when((peer < me) & (peer == 0))(clean_copy(peer).start)
+    for k, peer in far:
+        pl.when((peer < me))(clean_copy(peer).start)
+
+
     put(pga.at[me, clean], pgo.at[clean], po_sem.at[0], po_sem.at[2], head=other)
     drain(pga.at[pl.ds(0, half - 1), noisy], pg_s.at[0])
     drain(pga.at[pl.ds(0, n - 1), clean], pg_s.at[1])
@@ -464,15 +463,24 @@
     for at in range(m):
         gsum[at] = gw[at * slab : (at + 1) * slab]
         rp[at] = gw[at * slab : (at + 1) * slab].astype(jnp.bfloat16)
-    for peer in dp_peers:
-        put(rp.at[peer], rin.at[me_dp], rs_s.at[0], rs_r.at[dp_slot(me_dp, peer)], dp=peer)
+    parts = 2 if slab % 32 == 0 else 1
+
+    def slab_part(part):
+        return pl.ds(part * (slab // parts), slab // parts)
+
+    for part in range(parts):
+        span = slab_part(part)
+        for peer in dp_peers:
+            put(rp.at[peer, span], rin.at[me_dp, span], rs_s.at[0], rs_r.at[part, dp_slot(me_dp, peer)], dp=peer)
     drain(rp.at[pl.ds(0, m - 1)], rs_s.at[0])
     foreign_sum = foreign_own[...]
     for src in dp_peers:
         arrived(fin.at[src], rf_r.at[dp_slot(src, me_dp)])
         foreign_sum += fin[src].astype(jnp.float32)
     zout[...] = foreign_sum.astype(jnp.bfloat16)
-    put(zout, zin, z_sem.at[0], z_sem.at[1], context=partner)
+    for part in range(parts):
+        span = slab_part(part)
+        put(zout.at[span], zin.at[span], z_sem.at[0], z_sem.at[1 + part], context=partner)
     drain(zout, z_sem.at[0])
     arrived(wo, wo_sem.at[1])
     arrived(pgo.at[noisy], po_sem.at[1])
@@ -482,18 +490,23 @@
             dot_nt(pga[me], wf[head * half + at]) + dot_nt(pgo[...], wo[at])
         ).astype(jnp.bfloat16)
 
-    slab_sum = gsum[me_dp]
-    for src in dp_peers:
-        arrived(rin.at[src], rs_r.at[dp_slot(src, me_dp)])
-        slab_sum += rin[src].astype(jnp.float32)
-    arrived(zin, z_sem.at[1])
-    slab_sum += zin[...].astype(jnp.float32)
-    rall[me_dp] = slab_sum.astype(jnp.bfloat16)
-    for peer in dp_peers:
-        put(rall.at[me_dp], rall.at[me_dp], ra_s.at[0], ra_r.at[dp_slot(me_dp, peer)], dp=peer)
+    for part in range(parts):
+        span = slab_part(part)
+        slab_sum = gsum[me_dp, span]
+        for src in dp_peers:
+            arrived(rin.at[src, span], rs_r.at[part, dp_slot(src, me_dp)])
+            slab_sum += rin[src, span].astype(jnp.float32)
+        arrived(zin.at[span], z_sem.at[1 + part])
+        slab_sum += zin[span].astype(jnp.float32)
+        rall[me_dp, span] = slab_sum.astype(jnp.bfloat16)
+        for peer in dp_peers:
+            held = rall.at[me_dp, span]
+            put(held, held, ra_s.at[0], ra_r.at[part, dp_slot(me_dp, peer)], dp=peer)
     drain(rall.at[pl.ds(0, m - 1)], ra_s.at[0])
-    for src in dp_peers:
-        arrived(rall.at[src], ra_r.at[dp_slot(src, me_dp)])
+    for part in range(parts):
+        span = slab_part(part)
+        for src in dp_peers:
+            arrived(rall.at[src, span], ra_r.at[part, dp_slot(src, me_dp)])
     for at in range(m):
         gsum[at] = rall[at].astype(jnp.float32)
     gwk_ref[...] = gsum[: m // 2].reshape(HEAD_DIM, wrows).T
@@ -528,6 +541,8 @@
     bf16, f32 = jnp.bfloat16, jnp.float32
     vmem = pl.BlockSpec(memory_space=pltpu.VMEM)
     dma = pltpu.SemaphoreType.DMA
+    heads = q_width // HEAD_DIM
+    pack = math.gcd(heads, max(1, min(4, 2048 // (n * rows))))
     hbm = pl.BlockSpec(memory_space=pltpu.HBM)
     slab = pair // m
     results = (
@@ -537,7 +552,7 @@
         ((wrows, width), f32),
     )
     dq, gx, gwk, gwv = pl.pallas_call(
-        functools.partial(fused_kernel, n, m, share),
+        functools.partial(fused_kernel, n, m, share, pack),
         out_shape=tuple(pltpu.VMEM(*result) for result in results),
         in_specs=[pl.BlockSpec(memory_space=pltpu.SMEM)] + [hbm] * 5,
         out_specs=(vmem, vmem, vmem, vmem),
@@ -567,13 +582,13 @@
             pltpu.VMEM((slab, wrows), f32),
             pltpu.VMEM((slab, wrows), bf16),
             pltpu.VMEM((slab, wrows), bf16),
-            dma((4,)), pltpu.SemaphoreType.REGULAR, pltpu.SemaphoreType.REGULAR, pltpu.SemaphoreType.REGULAR, dma((2,)),
+            dma((4,)), pltpu.SemaphoreType.REGULAR, pltpu.SemaphoreType.REGULAR, dma((2,)),
             dma((n + 1,)), dma((n - 1, 2)), dma((direct_slots,)), dma((direct_slots,)),
             dma((n - 1,)), dma((n - 1, max(6, m - 1))), dma((2,)), dma((n - 1,)), dma((n - 1,)),
             dma((2,)), dma((2, half)), dma((2,)), dma((2, half)),
             dma((2,)), dma((2, half - 1)), dma((2,)), dma((2, half - 1)), dma((n - 1,)), dma((n - 1,)),
             dma((2,)), dma((half - 1,)), dma((n - 1,)), dma((3,)),
-            dma((1,)), dma((m - 1,)), dma((2,)), dma((1,)), dma((m - 1,)), dma((1,)), dma((m - 1,)),
+            dma((1,)), dma((m - 1,)), dma((3,)), dma((1,)), dma((2, m - 1)), dma((1,)), dma((2, m - 1)),
         ],
         compiler_params=pltpu.CompilerParams(
             collective_id=0, has_side_effects=True, vmem_limit_bytes=VMEM_LIMIT

time: 71.3 us -> 66.2 us (0.928)
  Pallas kernels: 69.9 us -> 64.6 us
    pallas_call x1, Pallas kernels: 68.3 us -> 63 us  [per_device(): pl.pallas_call(functools.partial(fused_kernel, n, m, share, pack), out_sh...]
where the time goes in v3:
time: 66.2 us; the launch traced here: 66 us
  Pallas kernels  64.6 us (98%)
  between operations  1.45 us (2%)
    pallas_call x1, Pallas kernels, per_device(): pl.pallas_call(functools.partial(fused_kernel, n, m, share, pack), out_sh...  63 us
    pallas_call x1, Pallas kernels, per_device(): pl.pallas_call(store_kernel, out_shape=tuple((jax.ShapeDtypeStruct(*resul...  1.52 us

profile of v3, /device:TPU:0, one launch (start us, length us, event | category | flops | bytes accessed | tf_op | source)
XLA Modules:
  0.0 66.0 jit_solution(4462406094010279675)
XLA Ops:
  1.3 63.0 %shard_map.93 = (bf16[256,1024]{1,0:T(8,128)(2,1)S(1)}, bf16[256,2048]{1,0:T(8,128)(2,1)S(1)}, f32[1024,128]{1,0:T(8,128)S(1)}, f32[1024,128]{1,0:T(8,128)S(1)}) custom-call(s32[1]{0:T(128)S(6)} %copy.10.blk_ref, bf16[256,2048]{1,0:T(8,128)(2,1)} %bitcast.5, bf16[256,1024]{1,0:T(8,128)(2,1)} %bitcast.6, bf16[256,1024]{1,0:T(8,128)(2,1)} %bitcast.7, ...), custom_call_target="tpu_custom_call" | custom-call | tf_op jit(solution)/shard_map/pallas_call | solution.py:554
  64.3 1.5 %shard_map.94 = (bf16[256,1024]{1,0:T(8,128)(2,1)}, bf16[256,2048]{1,0:T(8,128)(2,1)}, f32[1024,128]{1,0:T(8,128)}, f32[1024,128]{1,0:T(8,128)}) custom-call(bf16[256,1024]{1,0:T(8,128)(2,1)S(1)} %get-tuple-element.12.dq_in, bf16[256,2048]{1,0:T(8,128)(2,1)S(1)} %get-tuple-element.13.gx_in, f32[1024,128]{1,0:T(8,128)S(1)} %get-tuple-element.14.gwk_in, ...), custom_call_target="tpu_custom_call" | custom-call | tf_op jit(solution)/shard_map/pallas_call | solution.py:604

commit v4 on v3

--- a/solution.py
+++ b/solution.py
@@ -41,7 +41,7 @@
     dq_ref, gx_ref, gwk_ref, gwv_ref,
     qg, tokf, wf, wo, kv, kvn, kt, knt, dkv, dn, pgp, pin, pga, pgo, tokd, tokn,
     gsum, rp, rin, rall, fp, fin, foreign_own, zout, zin,
-    loc_sem, pair_sem, kv_credit, tok_sem, wz_s, wz_r, wd_s, wd_r, wx_s, wx_r, wo_sem, kv_s, kv_r,
+    loc_sem, pair_sem, kv_credit, sent_credit, tok_sem, wz_s, wz_r, wd_s, wd_r, wx_s, wx_r, wo_sem, kv_s, kv_r,
     t1_s, t1_r, f1_s, f1_r, t2_s, t2_r, f2_s, f2_r, pp_s, pp_r, pg_s, pn_r, pc_r, po_sem,
     rf_s, rf_r, z_sem, rs_s, rs_r, ra_s, ra_r,
 ):
@@ -86,14 +86,15 @@
     near = line_order(me, n)
     far = near[::-1]
     sides = (me + 1, me - 1)
-    dp_peers = [lax.rem(me_dp + off, m) for off in range(1, m)]
+    ring_peers = [lax.rem(me_dp + off, m) for off in range(1, m)]
+    dp_peers = [jnp.where(k < me_dp, k, k + 1) for k in range(m - 1)]
 
     two_step = m == 4 and share % 32 == 0
     if two_step:
         low = lax.rem(me_dp, 2)
         w_peers = [(0, me_dp + 1 - 2 * low), (1, lax.rem(me_dp + 2, 4))]
     else:
-        w_peers = list(enumerate(dp_peers))
+        w_peers = list(enumerate(ring_peers))
 
     w_copies = [
         pltpu.make_async_copy(wk_ref, wf.at[me, :, pl.ds(0, HEAD_DIM)], loc_sem.at[0]),
@@ -382,7 +383,6 @@
         pgp[block_at] = (dkv[block_at * rows : (block_at + 1) * rows] * pair_scale).astype(jnp.bfloat16)
     for k, peer in far:
         put_if(peer < me, pgp.at[peer], pin.at[me], pp_s.at[k - 1], pp_r.at[slot(me, peer)], context=peer)
-        drain(pgp.at[peer], pp_s.at[k - 1], peer < me)
 
 
     def clean_copy(peer):
@@ -425,6 +425,15 @@
     for peer in dp_peers:
         put(fp.at[peer], fin.at[me_dp], rf_s.at[0], rf_r.at[dp_slot(me_dp, peer)], dp=peer)
     drain(fp.at[pl.ds(0, m - 1)], rf_s.at[0])
+    for k, peer in near:
+        sent = copy_of(pgp.at[peer], pgp.at[peer], pp_s.at[k - 1], loc_sem.at[0], head=other)
+        pl.when(peer < me)(sent.wait_send)
+    for _, peer in near:
+
+        @pl.when((peer > me) & (me > 0))
+        def _(peer=peer):
+            pl.semaphore_signal(sent_credit, inc=1, device_id={"context": peer}, device_id_type=MESH)
+
     for k, src in near:
 
         @pl.when(src > me)
@@ -435,6 +444,11 @@
     pga[me, clean] = dkv[my_rows, :].astype(jnp.bfloat16)
     for k, peer in far:
         pl.when(peer > me)(clean_copy(peer).start)
+
+    @pl.when(me > 1)
+    def _():
+        pl.semaphore_wait(sent_credit, me - 1)
+
     for k, peer in far:
         pl.when((peer < me))(clean_copy(peer).start)
 
@@ -582,7 +596,7 @@
             pltpu.VMEM((slab, wrows), f32),
             pltpu.VMEM((slab, wrows), bf16),
             pltpu.VMEM((slab, wrows), bf16),
-            dma((4,)), pltpu.SemaphoreType.REGULAR, pltpu.SemaphoreType.REGULAR, dma((2,)),
+            dma((4,)), pltpu.SemaphoreType.REGULAR, pltpu.SemaphoreType.REGULAR, pltpu.SemaphoreType.REGULAR, dma((2,)),
             dma((n + 1,)), dma((n - 1, 2)), dma((direct_slots,)), dma((direct_slots,)),
             dma((n - 1,)), dma((n - 1, max(6, m - 1))), dma((2,)), dma((n - 1,)), dma((n - 1,)),
             dma((2,)), dma((2, half)), dma((2,)), dma((2, half)),

time: 66.2 us -> 65.5 us (0.989)
  Pallas kernels: 64.6 us -> 63.9 us
    pallas_call x1, Pallas kernels: 63 us -> 62.3 us  [per_device(): pl.pallas_call(functools.partial(fused_kernel, n, m, share, pack), out_sh...]
where the time goes in v4:
time: 65.5 us; the launch traced here: 65.3 us
  Pallas kernels  63.9 us (98%)
  between operations  1.45 us (2%)
    pallas_call x1, Pallas kernels, per_device(): pl.pallas_call(functools.partial(fused_kernel, n, m, share, pack), out_sh...  62.3 us
    pallas_call x1, Pallas kernels, per_device(): pl.pallas_call(store_kernel, out_shape=tuple((jax.ShapeDtypeStruct(*resul...  1.52 us

profile of v4, /device:TPU:0, one launch (start us, length us, event | category | flops | bytes accessed | tf_op | source)
XLA Modules:
  0.0 65.3 jit_solution(2160570322130146609)
XLA Ops:
  1.3 62.3 %shard_map.93 = (bf16[256,1024]{1,0:T(8,128)(2,1)S(1)}, bf16[256,2048]{1,0:T(8,128)(2,1)S(1)}, f32[1024,128]{1,0:T(8,128)S(1)}, f32[1024,128]{1,0:T(8,128)S(1)}) custom-call(s32[1]{0:T(128)S(6)} %copy.10.blk_ref, bf16[256,2048]{1,0:T(8,128)(2,1)} %bitcast.5, bf16[256,1024]{1,0:T(8,128)(2,1)} %bitcast.6, bf16[256,1024]{1,0:T(8,128)(2,1)} %bitcast.7, ...), custom_call_target="tpu_custom_call" | custom-call | tf_op jit(solution)/shard_map/pallas_call | solution.py:568
  63.6 1.5 %shard_map.94 = (bf16[256,1024]{1,0:T(8,128)(2,1)}, bf16[256,2048]{1,0:T(8,128)(2,1)}, f32[1024,128]{1,0:T(8,128)}, f32[1024,128]{1,0:T(8,128)}) custom-call(bf16[256,1024]{1,0:T(8,128)(2,1)S(1)} %get-tuple-element.12.dq_in, bf16[256,2048]{1,0:T(8,128)(2,1)S(1)} %get-tuple-element.13.gx_in, f32[1024,128]{1,0:T(8,128)S(1)} %get-tuple-element.14.gwk_in, ...), custom_call_target="tpu_custom_call" | custom-call | tf_op jit(solution)/shard_map/pallas_call | solution.py:618

commit v5 on v4

--- a/solution.py
+++ b/solution.py
@@ -304,6 +304,7 @@
                 lax.fori_loop(first, last, turn_of, 0)
 
     wide = pack * rows
+    exp2_scale = score_scale * math.log2(math.e)
 
     def head_turn(extent, turn, carry):
         open_rows = extent - step_rows
@@ -332,8 +333,8 @@
         peak = jnp.max(s, axis=0, keepdims=True)
         peak_own = jnp.maximum(peak[:, wide:], jnp.max(s_own, axis=0, keepdims=True))
         peak = jnp.concatenate([peak[:, :wide], peak_own], axis=1)
-        e = jnp.exp((s - peak) * score_scale)
-        e_own = jnp.exp((s_own - peak_own) * score_scale)
+        e = jnp.exp2((s - peak) * exp2_scale)
+        e_own = jnp.exp2((s_own - peak_own) * exp2_scale)
         total = jnp.sum(e, axis=0, keepdims=True)
         total_own = total[:, wide:] + jnp.sum(e_own, axis=0, keepdims=True)
         inverse = 1.0 / jnp.concatenate([total[:, :wide], total_own], axis=1)
@@ -376,12 +377,13 @@
     )
     clean, noisy = pl.ds(0, rows), pl.ds(rows, rows)
     pga[me, noisy] = (dn[...] * pair_scale).astype(jnp.bfloat16)
-    for peer in mates:
-        part = pga.at[me, noisy]
-        put(part, part, pg_s.at[0], pn_r.at[mate_slot(me, peer)], context=peer)
     for block_at in range(n):
         pgp[block_at] = (dkv[block_at * rows : (block_at + 1) * rows] * pair_scale).astype(jnp.bfloat16)
-    for k, peer in far:
+    for at, (k, peer) in enumerate(far):
+        if at == n - 2:
+            for mate in mates:
+                part = pga.at[me, noisy]
+                put(part, part, pg_s.at[0], pn_r.at[mate_slot(me, mate)], context=mate)
         put_if(peer < me, pgp.at[peer], pin.at[me], pp_s.at[k - 1], pp_r.at[slot(me, peer)], context=peer)
 
 
@@ -411,6 +413,15 @@
         mate_onward(src, 1)
     for src in cross:
         cross_onward(src, 0)
+    for k, peer in near:
+        sent = copy_of(pgp.at[peer], pgp.at[peer], pp_s.at[k - 1], loc_sem.at[0], head=other)
+        pl.when(peer < me)(sent.wait_send)
+    for _, peer in near:
+
+        @pl.when((peer > me) & (me > 0))
+        def _(peer=peer):
+            pl.semaphore_signal(sent_credit, inc=1, device_id={"context": peer}, device_id_type=MESH)
+
     foreign_side, foreign_columns = token_block(partner)
     gf = dot(pga[me, noisy].T, tokf[foreign_side, rows:, foreign_columns])
     for src in mates:
@@ -425,15 +436,6 @@
     for peer in dp_peers:
         put(fp.at[peer], fin.at[me_dp], rf_s.at[0], rf_r.at[dp_slot(me_dp, peer)], dp=peer)
     drain(fp.at[pl.ds(0, m - 1)], rf_s.at[0])
-    for k, peer in near:
-        sent = copy_of(pgp.at[peer], pgp.at[peer], pp_s.at[k - 1], loc_sem.at[0], head=other)
-        pl.when(peer < me)(sent.wait_send)
-    for _, peer in near:
-
-        @pl.when((peer > me) & (me > 0))
-        def _(peer=peer):
-            pl.semaphore_signal(sent_credit, inc=1, device_id={"context": peer}, device_id_type=MESH)
-
     for k, src in near:
 
         @pl.when(src > me)

time: 65.5 us -> 64.9 us (level)
  no operation moved by 1% of the time
where the time goes in v5:
time: 64.9 us; the launch traced here: 64.8 us
  Pallas kernels  63.3 us (98%)
  between operations  1.45 us (2%)
    pallas_call x1, Pallas kernels, per_device(): pl.pallas_call(functools.partial(fused_kernel, n, m, share, pack), out_sh...  61.8 us
    pallas_call x1, Pallas kernels, per_device(): pl.pallas_call(store_kernel, out_shape=tuple((jax.ShapeDtypeStruct(*resul...  1.52 us

profile of v5, /device:TPU:0, one launch (start us, length us, event | category | flops | bytes accessed | tf_op | source)
XLA Modules:
  0.0 64.8 jit_solution(10579770177011503644)
XLA Ops:
  1.3 61.8 %shard_map.93 = (bf16[256,1024]{1,0:T(8,128)(2,1)S(1)}, bf16[256,2048]{1,0:T(8,128)(2,1)S(1)}, f32[1024,128]{1,0:T(8,128)S(1)}, f32[1024,128]{1,0:T(8,128)S(1)}) custom-call(s32[1]{0:T(128)S(6)} %copy.10.blk_ref, bf16[256,2048]{1,0:T(8,128)(2,1)} %bitcast.5, bf16[256,1024]{1,0:T(8,128)(2,1)} %bitcast.6, bf16[256,1024]{1,0:T(8,128)(2,1)} %bitcast.7, ...), custom_call_target="tpu_custom_call" | custom-call | tf_op jit(solution)/shard_map/pallas_call | solution.py:570
  63.1 1.5 %shard_map.94 = (bf16[256,1024]{1,0:T(8,128)(2,1)}, bf16[256,2048]{1,0:T(8,128)(2,1)}, f32[1024,128]{1,0:T(8,128)}, f32[1024,128]{1,0:T(8,128)}) custom-call(bf16[256,1024]{1,0:T(8,128)(2,1)S(1)} %get-tuple-element.12.dq_in, bf16[256,2048]{1,0:T(8,128)(2,1)S(1)} %get-tuple-element.13.gx_in, f32[1024,128]{1,0:T(8,128)S(1)} %get-tuple-element.14.gwk_in, ...), custom_call_target="tpu_custom_call" | custom-call | tf_op jit(solution)/shard_map/pallas_call | solution.py:620

commit v6 on v5

--- a/solution.py
+++ b/solution.py
@@ -88,6 +88,8 @@
     sides = (me + 1, me - 1)
     ring_peers = [lax.rem(me_dp + off, m) for off in range(1, m)]
     dp_peers = [jnp.where(k < me_dp, k, k + 1) for k in range(m - 1)]
+    if m == 4:
+        dp_peers = [me_dp + 1 - 2 * lax.rem(me_dp, 2), lax.rem(me_dp + 2, 4), 3 - me_dp]
 
     two_step = m == 4 and share % 32 == 0
     if two_step:
@@ -165,8 +167,8 @@
         return pl.ds(pl.multiple_of(core * 2 * quarter + part * quarter, 16), quarter)
 
     def mate_rows(core, part):
-        if part == 0:
-            return pl.ds(pl.multiple_of(core * rows, 16), rows)
+        if part < 2:
+            return pl.ds(pl.multiple_of(core * rows + part * 2 * quarter, 16), 2 * quarter)
         return pl.ds(pl.multiple_of(core * 2 * quarter, 16), 2 * quarter)
 
     def cross_copy(part, peer):
@@ -178,14 +180,14 @@
         )
 
     def mate_copy(part, peer):
-        if part == 0:
+        if part < 2:
             side, columns = token_block(peer)
-            span = mate_rows(head, 0)
+            span = mate_rows(head, part)
             held = tokd.at[me, span]
         else:
             side, columns = token_block(lax.rem(peer + half, n))
             span = pl.ds(pl.multiple_of(rows + head * 2 * quarter, 16), 2 * quarter)
-            held = tokn.at[place, mate_rows(head, 1)]
+            held = tokn.at[place, mate_rows(head, 2)]
         return copy_of(
             tokf.at[side, span, columns], held,
             t2_s.at[part], t2_r.at[part, mate_slot(me, peer)], context=peer,
@@ -213,7 +215,7 @@
         if k == 1:
             arrived(tokf.at[other], tok_sem.at[1])
             for peer in mates:
-                for part in range(2):
+                for part in range(3):
                     pl.when(outer)(mate_copy(part, peer).start)
         if two_step and k > 1:
             w_forward(near[k - 2][1])
@@ -223,15 +225,17 @@
     for peer in cross[::-1]:
         pl.when(peer < me)(cross_copy(1, peer).start)
     for peer in mates:
-        pl.when(inner)(mate_copy(1, peer).start)
-        pl.when((peer < me) & inner)(mate_copy(0, peer).start)
+        pl.when(inner)(mate_copy(2, peer).start)
+        for part in range(2):
+            pl.when((peer < me) & inner)(mate_copy(part, peer).start)
     own_tokens = pltpu.make_async_copy(tokf.at[my_side, :, my_columns], tokd.at[me], loc_sem.at[3])
     own_tokens.start()
     for part in range(2):
         held = tokd.at[pl.ds(0, half), pl.ds(0, quarter)]
         drain(held, t1_s.at[part])
         drain(held, f1_s.at[part])
-    for part, held in enumerate((tokd.at[pl.ds(0, half - 1), pl.ds(0, rows)], tokn.at[pl.ds(0, half - 1), pl.ds(0, 2 * quarter)])):
+    for part in range(3):
+        held = tokn.at[pl.ds(0, half - 1), pl.ds(0, 2 * quarter)]
         drain(held, t2_s.at[part])
         drain(held, f2_s.at[part])
     if two_step:
@@ -290,6 +294,8 @@
         def _(peer=peer):
             pl.semaphore_signal(kv_credit, inc=1, device_id={"context": peer}, device_id_type=MESH)
 
+    for peer in mates:
+        pl.when((peer > me) & inner)(mate_copy(0, peer).start)
     kt[...] = kv[:, :HEAD_DIM].T
 
     steps = 4 if n % 4 == 0 else 1
@@ -392,7 +398,7 @@
         return copy_of(part, part, pg_s.at[1], pc_r.at[slot(me, peer)], context=peer)
 
     for peer in mates:
-        pl.when((peer > me) & inner)(mate_copy(0, peer).start)
+        pl.when((peer > me) & inner)(mate_copy(1, peer).start)
     put(pga.at[me, noisy], pgo.at[noisy], po_sem.at[0], po_sem.at[1], head=other)
     dkv[my_rows, :] *= pair_scale
 
@@ -402,7 +408,7 @@
         put(held, held, f1_s.at[part], f1_r.at[part, lax.rem(src, half)], head=other)
 
     def mate_held(src, core, part):
-        return tokd.at[src, mate_rows(core, 0)] if part == 0 else tokn.at[src - base, mate_rows(core, 1)]
+        return tokd.at[src, mate_rows(core, part)] if part < 2 else tokn.at[src - base, mate_rows(core, 2)]
 
     def mate_onward(src, part):
         held = mate_held(src, head, part)
@@ -410,12 +416,26 @@
         put(held, held, f2_s.at[part], f2_r.at[part, mate_slot(src, me)], head=other)
 
     for src in mates:
-        mate_onward(src, 1)
+        mate_onward(src, 2)
     for src in cross:
         cross_onward(src, 0)
+    def own_clean():
+        for k, src in near:
+
+            @pl.when(src > me)
+            def _(src=src):
+                arrived(pin.at[src], pp_r.at[slot(src, me)])
+                dkv[my_rows, :] += pin[src].astype(jnp.float32)
+
+        pga[me, clean] = dkv[my_rows, :].astype(jnp.bfloat16)
+        for k, peer in far:
+            pl.when(peer > me)(clean_copy(peer).start)
+
+    pl.when(me == 0)(own_clean)
     for k, peer in near:
         sent = copy_of(pgp.at[peer], pgp.at[peer], pp_s.at[k - 1], loc_sem.at[0], head=other)
-        pl.when(peer < me)(sent.wait_send)
+        pl.when((peer < me) & (me < n - 1))(sent.wait_send)
+        drain(pgp.at[peer], pp_s.at[k - 1], (peer < me) & (me == n - 1))
     for _, peer in near:
 
         @pl.when((peer > me) & (me > 0))
@@ -425,7 +445,7 @@
     foreign_side, foreign_columns = token_block(partner)
     gf = dot(pga[me, noisy].T, tokf[foreign_side, rows:, foreign_columns])
     for src in mates:
-        arrived(mate_held(src, other, 1), f2_r.at[1, mate_slot(src, me)])
+        arrived(mate_held(src, other, 2), f2_r.at[2, mate_slot(src, me)])
         arrived(pga.at[src, noisy], pn_r.at[mate_slot(src, me)])
         gf += dot(pga[src, noisy].T, tokn[src - base])
     slab = gf.shape[0] // m
@@ -436,16 +456,7 @@
     for peer in dp_peers:
         put(fp.at[peer], fin.at[me_dp], rf_s.at[0], rf_r.at[dp_slot(me_dp, peer)], dp=peer)
     drain(fp.at[pl.ds(0, m - 1)], rf_s.at[0])
-    for k, src in near:
-
-        @pl.when(src > me)
-        def _(src=src):
-            arrived(pin.at[src], pp_r.at[slot(src, me)])
-            dkv[my_rows, :] += pin[src].astype(jnp.float32)
-
-    pga[me, clean] = dkv[my_rows, :].astype(jnp.bfloat16)
-    for k, peer in far:
-        pl.when(peer > me)(clean_copy(peer).start)
+    pl.when(me > 0)(own_clean)
 
     @pl.when(me > 1)
     def _():
@@ -462,12 +473,14 @@
 
     own_tokens.wait()
     for src in mates:
-        mate_onward(src, 0)
+        for part in range(2):
+            mate_onward(src, part)
     for src in cross:
         cross_onward(src, 1)
     gw = dot(pga[me].T, tokd[me])
     for src in mates:
-        arrived(mate_held(src, other, 0), f2_r.at[0, mate_slot(src, me)])
+        for part in range(2):
+            arrived(mate_held(src, other, part), f2_r.at[part, mate_slot(src, me)])
         arrived(pga.at[src, clean], pc_r.at[slot(src, me)])
         gw += dot(pga[src].T, tokd[src])
     for src in cross:
@@ -602,7 +615,7 @@
             dma((n + 1,)), dma((n - 1, 2)), dma((direct_slots,)), dma((direct_slots,)),
             dma((n - 1,)), dma((n - 1, max(6, m - 1))), dma((2,)), dma((n - 1,)), dma((n - 1,)),
             dma((2,)), dma((2, half)), dma((2,)), dma((2, half)),
-            dma((2,)), dma((2, half - 1)), dma((2,)), dma((2, half - 1)), dma((n - 1,)), dma((n - 1,)),
+            dma((3,)), dma((3, half - 1)), dma((3,)), dma((3, half - 1)), dma((n - 1,)), dma((n - 1,)),
             dma((2,)), dma((half - 1,)), dma((n - 1,)), dma((3,)),
             dma((1,)), dma((m - 1,)), dma((3,)), dma((1,)), dma((2, m - 1)), dma((1,)), dma((2, m - 1)),
         ],

time: 64.9 us -> 64.7 us (level)
  no operation moved by 1% of the time
where the time goes in v6:
time: 64.7 us; the launch traced here: 64.6 us
  Pallas kernels  63.1 us (98%)
  between operations  1.45 us (2%)
    pallas_call x1, Pallas kernels, per_device(): pl.pallas_call(functools.partial(fused_kernel, n, m, share, pack), out_sh...  61.6 us
    pallas_call x1, Pallas kernels, per_device(): pl.pallas_call(store_kernel, out_shape=tuple((jax.ShapeDtypeStruct(*resul...  1.52 us

profile of v6, /device:TPU:0, one launch (start us, length us, event | category | flops | bytes accessed | tf_op | source)
XLA Modules:
  0.0 64.6 jit_solution(7197998346844540462)
XLA Ops:
  1.3 61.6 %shard_map.93 = (bf16[256,1024]{1,0:T(8,128)(2,1)S(1)}, bf16[256,2048]{1,0:T(8,128)(2,1)S(1)}, f32[1024,128]{1,0:T(8,128)S(1)}, f32[1024,128]{1,0:T(8,128)S(1)}) custom-call(s32[1]{0:T(128)S(6)} %copy.10.blk_ref, bf16[256,2048]{1,0:T(8,128)(2,1)} %bitcast.5, bf16[256,1024]{1,0:T(8,128)(2,1)} %bitcast.6, bf16[256,1024]{1,0:T(8,128)(2,1)} %bitcast.7, ...), custom_call_target="tpu_custom_call" | custom-call | tf_op jit(solution)/shard_map/pallas_call | solution.py:583
  62.9 1.5 %shard_map.94 = (bf16[256,1024]{1,0:T(8,128)(2,1)}, bf16[256,2048]{1,0:T(8,128)(2,1)}, f32[1024,128]{1,0:T(8,128)}, f32[1024,128]{1,0:T(8,128)}) custom-call(bf16[256,1024]{1,0:T(8,128)(2,1)S(1)} %get-tuple-element.12.dq_in, bf16[256,2048]{1,0:T(8,128)(2,1)S(1)} %get-tuple-element.13.gx_in, f32[1024,128]{1,0:T(8,128)S(1)} %get-tuple-element.14.gwk_in, ...), custom_call_target="tpu_custom_call" | custom-call | tf_op jit(solution)/shard_map/pallas_call | solution.py:633

commit v7 on v5

--- a/solution.py
+++ b/solution.py
@@ -88,6 +88,8 @@
     sides = (me + 1, me - 1)
     ring_peers = [lax.rem(me_dp + off, m) for off in range(1, m)]
     dp_peers = [jnp.where(k < me_dp, k, k + 1) for k in range(m - 1)]
+    if m == 4:
+        dp_peers = [me_dp + 1 - 2 * lax.rem(me_dp, 2), lax.rem(me_dp + 2, 4), 3 - me_dp]
 
     two_step = m == 4 and share % 32 == 0
     if two_step:

time: 64.9 us -> 64.7 us (level)
  no operation moved by 1% of the time
where the time goes in v7:
time: 64.7 us; the launch traced here: 64.4 us
  Pallas kernels  63 us (97%)
  between operations  1.45 us (2%)
    pallas_call x1, Pallas kernels, per_device(): pl.pallas_call(functools.partial(fused_kernel, n, m, share, pack), out_sh...  61.4 us
    pallas_call x1, Pallas kernels, per_device(): pl.pallas_call(store_kernel, out_shape=tuple((jax.ShapeDtypeStruct(*resul...  1.52 us

profile of v7, /device:TPU:0, one launch (start us, length us, event | category | flops | bytes accessed | tf_op | source)
XLA Modules:
  0.0 64.4 jit_solution(5399248787664211472)
XLA Ops:
  1.3 61.4 %shard_map.93 = (bf16[256,1024]{1,0:T(8,128)(2,1)S(1)}, bf16[256,2048]{1,0:T(8,128)(2,1)S(1)}, f32[1024,128]{1,0:T(8,128)S(1)}, f32[1024,128]{1,0:T(8,128)S(1)}) custom-call(s32[1]{0:T(128)S(6)} %copy.10.blk_ref, bf16[256,2048]{1,0:T(8,128)(2,1)} %bitcast.5, bf16[256,1024]{1,0:T(8,128)(2,1)} %bitcast.6, bf16[256,1024]{1,0:T(8,128)(2,1)} %bitcast.7, ...), custom_call_target="tpu_custom_call" | custom-call | tf_op jit(solution)/shard_map/pallas_call | solution.py:572
  62.7 1.5 %shard_map.94 = (bf16[256,1024]{1,0:T(8,128)(2,1)}, bf16[256,2048]{1,0:T(8,128)(2,1)}, f32[1024,128]{1,0:T(8,128)}, f32[1024,128]{1,0:T(8,128)}) custom-call(bf16[256,1024]{1,0:T(8,128)(2,1)S(1)} %get-tuple-element.12.dq_in, bf16[256,2048]{1,0:T(8,128)(2,1)S(1)} %get-tuple-element.13.gx_in, f32[1024,128]{1,0:T(8,128)S(1)} %get-tuple-element.14.gwk_in, ...), custom_call_target="tpu_custom_call" | custom-call | tf_op jit(solution)/shard_map/pallas_call | solution.py:622
